TPU v7x, 32 devices: a whole 2x2x4 slice. The times are simulated.
32 devices in a mesh: rows: 4 (over x, core), cols: 8 (over z, y).
Axes of the slice: x: 2, y: 2, z: 4, core: 2. Of those that a mesh axis runs over, the one named last changes fastest.
Arguments:
- elevation: float32 [512, 8192], P('rows', 'cols'), may hold values from -6 to 6
- data_mask: int32 [512, 8192], P('rows', 'cols'), may hold values 0 or 1
- tie_order: int32 [8], replicated, may hold values from 0 to 7, each once
Outputs:
- inflow: float32 [512, 8192], P('rows', 'cols')
Inputs may be any that keep to these rules, and one draw needn't show every extreme that they name: tie_order holds each of 0 to 7 once.
All inputs are finite; a program needn't handle non-finite values. No bound on the sum of `data_mask` on one device may be relied on, other than what follows from the above.
Results may differ from a plain program's by a relative error of at most 0.0003.
Values sent between devices are 32-bit elements; how exact they have to be, the bound alone decides.
A program may use at most 64 MiB of HBM per device.

v0:
```python
import functools

import jax
import jax.numpy as jnp
from jax import lax
from jax.experimental import pallas as pl
from jax.experimental.pallas import tpu as pltpu
from jax.sharding import PartitionSpec as P

ITERS = 8
OFFSETS = ((0, 1), (1, 1), (1, 0), (1, -1), (0, -1), (-1, -1), (-1, 0), (-1, 1))
RECIPROCAL = (1.0, 0.7071067811865476) * 4
RETENTION = 0.1
OUTSIDE = 1000.0
LANES = 128
F32 = jnp.float32


def coefficients(tie_ref):
    out = []
    for k in range(8):
        value = jnp.float32(0.0)
        for i in range(8):
            place = jnp.float32((1.0 + 0.5 * (7.0 - i) / 7.0) * RECIPROCAL[k])
            value = jnp.where(tie_ref[i] == k, place, value)
        out.append(value)
    return out


def shift_lanes(before, here, after, step, lane):
    if step == 0:
        return here
    if step < 0:
        return pltpu.roll(jnp.where(lane == LANES - 1, before, here), 1, 1)
    return pltpu.roll(jnp.where(lane == 0, after, here), LANES - 1, 1)


def take_lanes(values, index):
    return jnp.take_along_axis(values, index, axis=1, mode="promise_in_bounds")


def kernel(row_devices, col_devices, tie_hbm, elev_ref, mask_ref, out_ref, tie_ref, zp, zl, zr, mask, recip, rl, rr, parts, ones,
           coarse, side, srecv, vrecv, load_sem, tie_sem, send_sem, recv_sem):
    rows, cols = elev_ref.shape
    groups, blocks = rows // 8, cols // LANES
    crows = groups
    row, col = lax.axis_index("rows"), lax.axis_index("cols")
    ring, rim = 0, blocks + 1

    loads = []
    for j in range(blocks):
        part = pl.ds(j * LANES, LANES)
        loads.append((
            pltpu.make_async_copy(elev_ref.at[:, part], zp.at[j + 1, pl.ds(8, rows), :], load_sem.at[j]),
            pltpu.make_async_copy(mask_ref.at[:, part], mask.at[j], load_sem.at[blocks + j])))
        loads[-1][0].start()
        loads[-1][1].start()
    tie_load = pltpu.make_async_copy(tie_hbm, tie_ref, tie_sem)
    tie_load.start()

    barrier = pltpu.get_barrier_semaphore()
    exists = []
    for step_row, step_col in OFFSETS:
        there = jnp.bool_(True)
        if step_row > 0:
            there = row < row_devices - 1
        if step_row < 0:
            there = row > 0
        if step_col > 0:
            there = jnp.logical_and(there, col < col_devices - 1)
        if step_col < 0:
            there = jnp.logical_and(there, col > 0)
        exists.append(there)

    def peer(k):
        return {"rows": row + OFFSETS[k][0], "cols": col + OFFSETS[k][1]}

    for k in range(8):
        @pl.when(exists[k])
        def _():
            pl.semaphore_signal(barrier, inc=1, device_id=peer(k), device_id_type=pl.DeviceIdType.MESH)

    lane = lax.broadcasted_iota(jnp.int32, (8, LANES), 1)
    sub = lax.broadcasted_iota(jnp.int32, (8, LANES), 0)
    lane_c = lax.broadcasted_iota(jnp.int32, (crows, LANES), 1)
    middle_lanes = jnp.logical_and(lane_c >= LANES // 4, lane_c < 3 * LANES // 4)

    SIDES, UPDOWN = (0, 1, 3, 4, 5, 7), (2, 6)

    def halo_rows(k):
        return zp.at[pl.ds(1, blocks), pl.ds(8 + rows if k == 2 else 0, 8), :]

    def edge_rows(k):
        return zp.at[pl.ds(1, blocks), pl.ds(rows if k == 2 else 8, 8), :]

    for k in range(8):
        @pl.when(jnp.logical_not(exists[k]))
        def _():
            if k in UPDOWN:
                region = halo_rows(k)
                region[...] = jnp.full(region.shape, OUTSIDE, F32)
                vrecv[k // 4, 0:crows, :] = jnp.full((crows, LANES), OUTSIDE, F32)
                vrecv[k // 4, crows:2 * crows, :] = jnp.zeros((crows, LANES), F32)
            else:
                srecv[k, 0:crows, :] = jnp.where(middle_lanes, 0.0, OUTSIDE)
                srecv[k, crows:crows + 8, :] = jnp.full((8, LANES), OUTSIDE, F32)

    ones[...] = (
        lax.broadcasted_iota(jnp.int32, (cols, LANES), 0) // 8 == lax.broadcasted_iota(jnp.int32, (cols, LANES), 1)
    ).astype(F32).astype(jnp.bfloat16)

    total = jnp.zeros((4 * crows, LANES), F32)
    for j in range(blocks):
        loads[j][0].wait()
        loads[j][1].wait()
        height_sum = jnp.zeros((crows, LANES), F32)
        count_sum = jnp.zeros((crows, LANES), F32)
        for s in range(8):
            valid = mask[j, pl.ds(s, crows, stride=8), :].astype(F32)
            height_sum = height_sum + valid * zp[j + 1, pl.ds(8 + s, crows, stride=8), :]
            count_sum = count_sum + valid
        high = height_sum.astype(jnp.bfloat16)
        rest = height_sum - high.astype(F32)
        middle = rest.astype(jnp.bfloat16)
        low = (rest - middle.astype(F32)).astype(jnp.bfloat16)
        stacked = jnp.concatenate([count_sum.astype(jnp.bfloat16), high, middle, low], axis=0)
        total = total + jnp.dot(stacked, ones[j * LANES:(j + 1) * LANES, :], preferred_element_type=F32)
    counts = total[0:crows]
    heights = total[crows:2 * crows] + (total[2 * crows:3 * crows] + total[3 * crows:])
    overview = heights / (counts + 1.0)
    runoff = counts * (1.0 / 64.0)

    packed = jnp.zeros((8, LANES), F32)
    for g in range(groups):
        at = pl.ds(8 + 8 * g, 8)
        edges = jnp.where(lane < LANES // 2, zp[1, at, :], zp[blocks, at, :])
        zp[rim, at, :] = edges
        packed = jnp.where(lane // 4 == g, pltpu.roll(edges, (2 + 4 * g) % LANES, 1), packed)
    side[crows:crows + 8, :] = packed
    side[0:crows, :] = jnp.where(middle_lanes, pltpu.roll(runoff, LANES // 2, 1), overview)
    coarse[0:crows, :] = overview
    coarse[crows:2 * crows, :] = runoff

    pl.semaphore_wait(barrier, functools.reduce(jnp.add, [there.astype(jnp.int32) for there in exists]))

    def copies(k, arriving=False):
        slot = k if arriving else (k + 4) % 8

        def remote(src, dst, extra):
            return pltpu.make_async_remote_copy(
                src_ref=src, dst_ref=dst, send_sem=send_sem.at[k + extra], recv_sem=recv_sem.at[slot + extra],
                device_id=peer(k), device_id_type=pl.DeviceIdType.MESH)

        if k in UPDOWN:
            return remote(edge_rows(k), halo_rows(slot), 8), remote(coarse, vrecv.at[slot // 4], 0)
        fine, wide = pl.ds(crows, 8), pl.ds(0, crows)
        return (remote(side.at[fine, :], srecv.at[slot, fine, :], 8),
                remote(side.at[wide, :], srecv.at[slot, wide, :], 0))

    for which in range(2):
        for k in (1, 3, 5, 7, 0, 4, 2, 6):
            @pl.when(exists[k])
            def _():
                copies(k)[which].start()

    tie_load.wait()
    coef = coefficients(tie_ref)

    def beside_heights(at, around):
        for j, before, after in around:
            line = [zp[b, at, :] for b in (before, j, after)]
            zl[j, at, :] = shift_lanes(*line, -1, lane)
            zr[j, at, :] = shift_lanes(*line, 1, lane)

    by_column = {-1: zl, 0: zp, 1: zr}
    scale_by_column = {-1: rl, 0: recip, 1: rr}

    def first_pass(g, around):
        done = {}
        middle_at = pl.ds(8 * g + 7, 8)
        for j, before, after in around:
            here = zp[j, middle_at, :]
            summed = jnp.full((8, LANES), RETENTION, F32)
            for k, (off_row, off_col) in enumerate(OFFSETS):
                beside = by_column[off_col][j, pl.ds(8 * g + 7 + off_row, 8), :]
                summed = summed + coef[k] * jnp.maximum(here - beside, 0.0)
            done[j] = 1.0 / summed
            recip[j, middle_at, :] = done[j]
        for j, before, after in around:
            line = [done.get(b, done[j]) for b in (before, j, after)]
            rl[j, middle_at, :] = shift_lanes(*line, -1, lane)
            rr[j, middle_at, :] = shift_lanes(*line, 1, lane)

    def second_pass(g, around, store):
        for j, before, after in around:
            here = zp[j, pl.ds(8 * g + 8, 8), :]
            inside, outer = {}, {}
            for step_col in (-1, 0, 1):
                terms = {}
                for step_row in (-1, 0, 1):
                    if (step_row, step_col) == (0, 0):
                        continue
                    k = OFFSETS.index((-step_row, -step_col))
                    at = pl.ds(8 * g + 8 + step_row, 8)
                    source = by_column[step_col][j, at, :]
                    scale = scale_by_column[step_col][j, at, :]
                    terms[step_row] = coef[k] * jnp.maximum(source - here, 0.0) * scale
                inside[step_col] = jnp.where(sub == 0, 0.0, terms[-1]) + jnp.where(sub == 7, 0.0, terms[1])
                if step_col != 0:
                    inside[step_col] = inside[step_col] + terms[0]
                outer[step_col] = jnp.where(sub == 0, terms[-1], jnp.where(sub == 7, terms[1], 0.0))
            first, last = (lane & 7) == 0, (lane & 7) == 7
            for number, field in enumerate((inside, outer)):
                store(g, j, 2 * number, field[0] + jnp.where(first, 0.0, field[-1]) + jnp.where(last, 0.0, field[1]))
                store(g, j, 2 * number + 1, jnp.where(first, field[-1], jnp.where(last, field[1], 0.0)))

    def keep(g, j, number, value):
        parts[number, j - 1, pl.ds(8 * g, 8), :] = value

    def keep_edges(g, j, number, value):
        at = pl.ds(8 * g, 8)
        parts[number, 0, at, :] = jnp.where(lane < 8, value, parts[number, 0, at, :])
        parts[number, blocks - 1, at, :] = jnp.where(lane >= LANES - 8, value, parts[number, blocks - 1, at, :])

    own = [(j, j - 1, j + 1 if j < blocks else ring) for j in range(1, blocks + 1)]
    outside, edges = (ring, blocks, 1), (rim, ring, ring)

    def loop(start, stop, body):
        def step(g, carry):
            body(g)
            return carry

        lax.fori_loop(start, stop, step, 0)

    loop(0, groups, lambda g: beside_heights(pl.ds(pl.multiple_of(8 * g + 8, 8), 8), own))
    loop(1, groups, lambda g: first_pass(g, own))
    loop(1, groups - 1, lambda g: second_pass(g, own, keep))

    def receive(which):
        for k in range(8):
            @pl.when(exists[k])
            def _():
                copies(k, arriving=True)[which].wait_recv()

    receive(0)

    def outside_columns(g, right, left):
        chosen = jnp.where(lane >= 4 * g + 2, srecv[right, crows:crows + 8, :], srecv[left, crows:crows + 8, :])
        return pltpu.roll(chosen, (2 * LANES - 4 * g - 2) % LANES, 1)

    for g in range(groups):
        zp[ring, pl.ds(8 + 8 * g, 8), :] = outside_columns(g, 0, 4)
    zp[ring, 0:8, :] = outside_columns(groups - 1, 7, 5)
    zp[ring, rows + 8:rows + 16, :] = outside_columns(0, 1, 3)
    for at in (0, rows + 8):
        zp[rim, at:at + 8, :] = jnp.where(lane < LANES // 2, zp[1, at:at + 8, :], zp[blocks, at:at + 8, :])
    for at in (0, rows + 8):
        beside_heights(pl.ds(at, 8), own)
    loop(0, groups + 2, lambda g: beside_heights(pl.ds(pl.multiple_of(8 * g, 8), 8), [outside, edges]))
    loop(0, groups + 1, lambda g: first_pass(g, [outside, edges]))
    loop(0, 2, lambda i: first_pass(i * groups, own))
    loop(0, 2, lambda i: second_pass(i * (groups - 1), own, keep))
    loop(0, groups, lambda g: second_pass(g, [edges], keep_edges))

    receive(1)

    half = LANES // 2

    def window(field):
        def beside(right, left):
            a, b = srecv[right, 0:crows, :], srecv[left, 0:crows, :]
            return jnp.where(lane_c < half, a, b) if field == 0 else pltpu.roll(jnp.where(lane_c < half, b, a), half, 1)

        at = slice(field * crows, (field + 1) * crows)
        here = jnp.concatenate([coarse[at, :], beside(0, 4)], axis=1)
        below = jnp.concatenate([vrecv[0, at, :], beside(1, 3)], axis=1)
        above = jnp.concatenate([vrecv[1, at, :], beside(7, 5)], axis=1)
        sub_w = lax.broadcasted_iota(jnp.int32, (8, 2 * LANES), 0)
        mixed = jnp.where(sub_w < 4, below[8:16], above[crows - 16:crows - 8])
        return jnp.concatenate([here, below[0:8], mixed, above[crows - 8:crows]], axis=0)

    z = window(0)
    supply = window(1)
    high = z.shape[0]

    def turn(x, step, axis):
        return x if step == 0 else pltpu.roll(x, (-step) % x.shape[axis], axis)

    turned = {step: turn(z, step, 1) for step in (-1, 0, 1)}
    slopes = []
    for k, (step_row, step_col) in enumerate(OFFSETS):
        slopes.append(coef[k] * jnp.maximum(z - turn(turned[step_col], step_row, 0), 0.0))
    share = 1.0 / (functools.reduce(jnp.add, slopes) + RETENTION)
    weight = {}
    for k, (step_row, step_col) in enumerate(OFFSETS):
        weight[step_row, step_col] = turn(slopes[k] * share, -step_col, 1)
    flow = supply
    for _ in range(ITERS):
        moved = {step: turn(flow, -step, 1) for step in (-1, 0, 1)}
        sums = {}
        for step_row in (-1, 0, 1):
            sums[step_row] = functools.reduce(
                jnp.add, [weight[step_row, c] * moved[c] for c in (-1, 0, 1) if (step_row, c) in weight])
        flow = supply + sums[0] + turn(sums[1], -1, 0) + turn(sums[-1], 1, 0)

    left = turn(flow, -1, 1)[:, :LANES]
    right = turn(flow, 1, 1)[:, :LANES]
    centre = flow[:, :LANES]
    first, last = (lane & 7) == 0, (lane & 7) == 7
    per_block = LANES // 8
    for j in range(blocks):
        index = lane // 8 + j * per_block
        spread = []
        for at in list(range(0, crows, 8)) + [crows, high - 8]:
            mid = take_lanes(centre[at:at + 8], index)
            beside = jnp.where(first, take_lanes(left[at:at + 8], index), take_lanes(right[at:at + 8], index))
            spread.append((mid, beside))
        for g in range(groups):
            def level(number, group):
                where_at = {-1: (len(spread) - 1, 7), groups: (len(spread) - 2, 0)}.get(group, (group // 8, group % 8))
                line = spread[where_at[0]][number][where_at[1]:where_at[1] + 1, :]
                return jnp.broadcast_to(line, (8, LANES))

            at = slice(8 * g, 8 * g + 8)
            value = mask[j, at, :].astype(F32)
            for number in range(2):
                value = value + parts[number, j, at, :] * level(number, g)
                across = jnp.where(sub == 0, level(number, g - 1), level(number, g + 1))
                value = value + parts[2 + number, j, at, :] * across
            out_ref[at, j * LANES:(j + 1) * LANES] = value

    for k in range(8):
        @pl.when(exists[k])
        def _():
            for copy in copies(k):
                copy.wait_send()


def solution(mesh):
    row_devices, col_devices = mesh.shape["rows"], mesh.shape["cols"]

    def on_device(elevation, data_mask, tie_order):
        rows, cols = elevation.shape
        groups, blocks = rows // 8, cols // LANES
        return pl.pallas_call(
            functools.partial(kernel, row_devices, col_devices),
            out_shape=pltpu.VMEM((rows, cols), F32),
            in_specs=[pl.BlockSpec(memory_space=pl.ANY)] * 3,
            out_specs=pl.BlockSpec(memory_space=pltpu.VMEM),
            scratch_shapes=[
                pltpu.SMEM((8,), jnp.int32),
                pltpu.VMEM((blocks + 2, rows + 16, LANES), F32),
                pltpu.VMEM((blocks + 2, rows + 16, LANES), F32),
                pltpu.VMEM((blocks + 2, rows + 16, LANES), F32),
                pltpu.VMEM((blocks, rows, LANES), jnp.int32),
                pltpu.VMEM((blocks + 2, rows + 16, LANES), F32),
                pltpu.VMEM((blocks + 2, rows + 16, LANES), F32),
                pltpu.VMEM((blocks + 2, rows + 16, LANES), F32),
                pltpu.VMEM((4, blocks, rows, LANES), F32),
                pltpu.VMEM((cols, LANES), jnp.bfloat16),
                pltpu.VMEM((2 * groups, LANES), F32),
                pltpu.VMEM((groups + 8, LANES), F32),
                pltpu.VMEM((8, groups + 8, LANES), F32),
                pltpu.VMEM((2, 2 * groups, LANES), F32),
                pltpu.SemaphoreType.DMA((2 * blocks,)),
                pltpu.SemaphoreType.DMA,
                pltpu.SemaphoreType.DMA((16,)),
                pltpu.SemaphoreType.DMA((16,)),
            ],
            compiler_params=pltpu.CompilerParams(collective_id=0, has_side_effects=True, vmem_limit_bytes=61000000),
        )(tie_order, elevation, data_mask)

    return jax.shard_map(
        on_device, mesh=mesh, in_specs=(P("rows", "cols"), P("rows", "cols"), P()),
        out_specs=P("rows", "cols"), check_vma=False)
```

profile of v0, /device:TPU:1, one launch (start us, length us, event | category | flops | bytes accessed | tf_op | source)
XLA Modules:
  0.0 14.0 jit_solution(6516077938258451737)
XLA Ops:
  0.0 13.2 %shard_map.37 = f32[128,1024]{1,0:T(8,128)S(1)} custom-call(s32[8]{0:T(128)} %tie_hbm.1, f32[128,1024]{1,0:T(8,128)} %elev_ref.1, s32[128,1024]{1,0:T(8,128)} %mask_ref.1), custom_call_target="tpu_custom_call" | custom-call | tf_op jit(solution)/shard_map/pallas_call | solution.py:345
  13.2 0.8 %copy.5 = f32[128,1024]{1,0:T(8,128)} copy(f32[128,1024]{1,0:T(8,128)S(1)} %shard_map.37) | data formatting | bytes 1048576
where the time goes:
time: 14.1 us; the launch traced here: 14 us
  Pallas kernels  13.2 us (94%)
  local copies, waits for them, and re-layouts  0.8 us (6%)
    pallas_call x1, Pallas kernels, on_device(): pl.pallas_call(functools.partial(kernel, row_devices, col_devices), out_s...  13.2 us
    unnamed x1, local copies, waits for them, and re-layouts  0.8 us

commit v1 on v0

v1 whole, which is shorter than its diff:
```python
import functools

import jax
import jax.numpy as jnp
from jax import lax
from jax.experimental import pallas as pl
from jax.experimental.pallas import tpu as pltpu
from jax.sharding import PartitionSpec as P

ITERS = 8
OFFSETS = ((0, 1), (1, 1), (1, 0), (1, -1), (0, -1), (-1, -1), (-1, 0), (-1, 1))
RECIPROCAL = (1.0, 0.7071067811865476) * 4
RETENTION = 0.1
OUTSIDE = 1000.0
LANES = 128
F32 = jnp.float32


def coefficients(tie_ref):
    out = []
    for k in range(8):
        value = jnp.float32(0.0)
        for i in range(8):
            place = jnp.float32((1.0 + 0.5 * (7.0 - i) / 7.0) * RECIPROCAL[k])
            value = jnp.where(tie_ref[i] == k, place, value)
        out.append(value)
    return out


def shift_lanes(before, here, after, step, lane):
    if step == 0:
        return here
    if step < 0:
        return pltpu.roll(jnp.where(lane == LANES - 1, before, here), 1, 1)
    return pltpu.roll(jnp.where(lane == 0, after, here), LANES - 1, 1)


def take_lanes(values, index):
    return jnp.take_along_axis(values, index, axis=1, mode="promise_in_bounds")


def kernel(row_devices, col_devices, tie_hbm, elev_ref, mask_ref, out_ref, tie_ref, zp, zl, zr, mask, recip, pending, base, inner, outer,
           inner_edge, outer_edge, turned, ones, side, tall, srecv, vrecv, load_sem, tie_sem, send_sem, recv_sem):
    rows, cols = elev_ref.shape
    groups, blocks = rows // 8, cols // LANES
    crows, halves = groups, groups // 8
    row, col = lax.axis_index("rows"), lax.axis_index("cols")
    far = blocks - 1

    loads = {}
    for j in [0, far] + list(range(1, far)):
        part = pl.ds(j * LANES, LANES)
        loads[j] = (
            pltpu.make_async_copy(elev_ref.at[:, part], zp.at[j, pl.ds(8, rows), :], load_sem.at[j]),
            pltpu.make_async_copy(mask_ref.at[:, part], mask.at[j], load_sem.at[blocks + j]))
        loads[j][0].start()
        loads[j][1].start()
    tie_load = pltpu.make_async_copy(tie_hbm, tie_ref, tie_sem)
    tie_load.start()

    barrier = pltpu.get_barrier_semaphore()
    exists = []
    for step_row, step_col in OFFSETS:
        there = jnp.bool_(True)
        if step_row > 0:
            there = row < row_devices - 1
        if step_row < 0:
            there = row > 0
        if step_col > 0:
            there = jnp.logical_and(there, col < col_devices - 1)
        if step_col < 0:
            there = jnp.logical_and(there, col > 0)
        exists.append(there)

    def peer(k):
        return {"rows": row + OFFSETS[k][0], "cols": col + OFFSETS[k][1]}

    for k in range(8):
        @pl.when(exists[k])
        def _():
            pl.semaphore_signal(barrier, inc=1, device_id=peer(k), device_id_type=pl.DeviceIdType.MESH)

    lane = lax.broadcasted_iota(jnp.int32, (8, LANES), 1)
    sub = lax.broadcasted_iota(jnp.int32, (8, LANES), 0)
    lane_c = lax.broadcasted_iota(jnp.int32, (crows, LANES), 1)
    middle_lanes = jnp.logical_and(lane_c >= LANES // 4, lane_c < 3 * LANES // 4)
    first, last = (lane & 7) == 0, (lane & 7) == 7
    half = LANES // 2
    nothing = jnp.zeros((8, LANES), F32)

    SIDES, UPDOWN = (0, 1, 3, 4, 5, 7), (2, 6)

    ones[...] = (
        lax.broadcasted_iota(jnp.int32, (cols, LANES), 0) // 8 == lax.broadcasted_iota(jnp.int32, (cols, LANES), 1)
    ).astype(F32).astype(jnp.bfloat16)

    loads[0][0].wait()
    loads[far][0].wait()
    ends = jnp.where(lax.broadcasted_iota(jnp.int32, (rows, LANES), 1) < half, zp[0, 8:8 + rows, :], zp[far, 8:8 + rows, :])
    ends = jnp.transpose(ends)
    tile = jnp.where(sub < 4, pltpu.roll(ends[0:8], 2, 0), pltpu.roll(ends[LANES - 8:LANES], 6, 0))
    side[crows:crows + 8, :] = tile
    tall[16 + 2 * crows:24 + 2 * crows, :] = tile

    total = jnp.zeros((4 * crows, LANES), F32)
    for j in loads:
        if j not in (0, far):
            loads[j][0].wait()
        loads[j][1].wait()
        height_sum = jnp.zeros((crows, LANES), F32)
        count_sum = jnp.zeros((crows, LANES), F32)
        for s in range(8):
            valid = mask[j, pl.ds(s, crows, stride=8), :].astype(F32)
            height_sum = height_sum + valid * zp[j, pl.ds(8 + s, crows, stride=8), :]
            count_sum = count_sum + valid
        high = height_sum.astype(jnp.bfloat16)
        rest = height_sum - high.astype(F32)
        middle = rest.astype(jnp.bfloat16)
        low = (rest - middle.astype(F32)).astype(jnp.bfloat16)
        stacked = jnp.concatenate([count_sum.astype(jnp.bfloat16), high, middle, low], axis=0)
        total = total + jnp.dot(stacked, ones[j * LANES:(j + 1) * LANES, :], preferred_element_type=F32)
        for number, at in enumerate((8, 9, rows + 6, rows + 7)):
            line = (0, 8, 24 + 2 * crows, 32 + 2 * crows)[number]
            tall[line + j:line + j + 1, :] = zp[j, at:at + 1, :]
    counts = total[0:crows]
    heights = total[crows:2 * crows] + (total[2 * crows:3 * crows] + total[3 * crows:])
    overview = heights / (counts + 1.0)
    runoff = counts * (1.0 / 64.0)
    side[0:crows, :] = jnp.where(middle_lanes, pltpu.roll(runoff, half, 1), overview)
    tall[16:16 + crows, :] = overview
    tall[16 + crows:16 + 2 * crows, :] = runoff

    pl.semaphore_wait(barrier, functools.reduce(jnp.add, [there.astype(jnp.int32) for there in exists]))

    def copies(k, arriving=False):
        slot = k if arriving else (k + 4) % 8
        if k in UPDOWN:
            src, dst = tall.at[pl.ds(16 if k == 2 else 0, 24 + 2 * crows), :], vrecv.at[slot // 4]
        else:
            src, dst = side, srecv.at[slot]
        return pltpu.make_async_remote_copy(
            src_ref=src, dst_ref=dst, send_sem=send_sem.at[k], recv_sem=recv_sem.at[slot],
            device_id=peer(k), device_id_type=pl.DeviceIdType.MESH)

    for k in (1, 3, 5, 7, 0, 4, 2, 6):
        @pl.when(exists[k])
        def _():
            copies(k).start()

    for k in range(8):
        @pl.when(jnp.logical_not(exists[k]))
        def _():
            if k in UPDOWN:
                for at in range(0, 24 + 2 * crows, 8):
                    start = 16 + crows if k == 2 else crows
                    vrecv[k // 4, at:at + 8, :] = jnp.full((8, LANES), 0.0 if start <= at < start + crows else OUTSIDE, F32)
            else:
                srecv[k, 0:crows, :] = jnp.where(middle_lanes, 0.0, OUTSIDE)
                srecv[k, crows:crows + 8, :] = jnp.full((8, LANES), OUTSIDE, F32)

    tie_load.wait()
    coef = coefficients(tie_ref)

    for g in range(groups):
        at = pl.ds(8 * g + 8, 8)
        for j in range(blocks):
            here = zp[j, at, :]
            before, after = zp[(j - 1) % blocks, at, :], zp[(j + 1) % blocks, at, :]
            zl[j, at, :] = shift_lanes(before, here, after, -1, lane)
            zr[j, at, :] = shift_lanes(before, here, after, 1, lane)
            base[j, pl.ds(8 * g, 8), :] = mask[j, pl.ds(8 * g, 8), :].astype(F32)

    by_column = {-1: zl, 0: zp, 1: zr}

    def within(j, share):
        if j == 0:
            share = jnp.where(lane == 0, 0.0, share)
        if j == far:
            share = jnp.where(lane == LANES - 1, 0.0, share)
        return share

    def leaving(g, j):
        here = zp[j, pl.ds(8 * g + 8, 8), :]
        slopes = {}
        for k, (off_row, off_col) in enumerate(OFFSETS):
            beside = by_column[off_col][j, pl.ds(8 * g + 8 + off_row, 8), :]
            slopes[off_row, off_col] = coef[k] * jnp.maximum(here - beside, 0.0)
        share = within(j, 1.0 / (functools.reduce(jnp.add, slopes.values()) + RETENTION))
        recip[j, pl.ds(8 * g + 8, 8), :] = share
        down, up = jnp.where(sub == 7, 0.0, share), jnp.where(sub == 0, 0.0, share)
        out = []
        for c in (-1, 0, 1):
            moved = pltpu.roll(slopes[1, c] * down, 1, 0) + pltpu.roll(slopes[-1, c] * up, 7, 0)
            out.append(moved if c == 0 else moved + slopes[0, c] * share)
        return out

    def across(fields, j):
        west = fields[j - 1][2] if j > 0 else nothing
        east = fields[j + 1][0] if j < far else nothing
        from_west = pltpu.roll(jnp.where(lane == LANES - 1, west, fields[j][2]), 1, 1)
        from_east = pltpu.roll(jnp.where(lane == 0, east, fields[j][0]), LANES - 1, 1)
        kept = fields[j][1] + jnp.where(first, 0.0, from_west) + jnp.where(last, 0.0, from_east)
        return kept, jnp.where(first, from_west, jnp.where(last, from_east, 0.0))

    def settle(g, fields):
        for j in range(blocks):
            inner[j, pl.ds(8 * g, 8), :], outer[j, pl.ds(8 * g, 8), :] = across(fields, j)

    pending[...] = jnp.zeros(pending.shape, F32)

    def step(g, carry):
        fields = [[pending[j, c] for c in range(3)] for j in range(blocks)]
        settle(g - 1, fields)
        for j in range(blocks):
            for c, value in enumerate(leaving(g, j)):
                pending[j, c] = value
        return carry

    lax.fori_loop(1, groups - 1, step, 0)
    settle(groups - 2, [[pending[j, c] for c in range(3)] for j in range(blocks)])

    for k in range(8):
        @pl.when(exists[k])
        def _():
            copies(k, arriving=True).wait_recv()

    def turn(x, step, axis):
        return x if step == 0 else pltpu.roll(x, (-step) % x.shape[axis], axis)

    coarse_at = (16, 0)
    tile_at = (16 + 2 * crows, 2 * crows)
    line_at = (0, 24 + 2 * crows - 16)

    def window(field):
        def beside(right, left):
            a, b = srecv[right, 0:crows, :], srecv[left, 0:crows, :]
            return jnp.where(lane_c < half, a, b) if field == 0 else pltpu.roll(jnp.where(lane_c < half, b, a), half, 1)

        def level(slot):
            return vrecv[slot, coarse_at[slot] + field * crows:coarse_at[slot] + (field + 1) * crows, :]

        here = jnp.concatenate([tall[16 + field * crows:16 + (field + 1) * crows, :], beside(0, 4)], axis=1)
        below = jnp.concatenate([level(0), beside(1, 3)], axis=1)
        above = jnp.concatenate([level(1), beside(7, 5)], axis=1)
        sub_w = lax.broadcasted_iota(jnp.int32, (8, 2 * LANES), 0)
        mixed = jnp.where(sub_w < 4, below[8:16], above[crows - 16:crows - 8])
        return jnp.concatenate([here, below[0:8], mixed, above[crows - 8:crows]], axis=0)

    def shares(z):
        beside_rows = {step: turn(z, step, 1) for step in (-1, 0, 1)}
        return beside_rows

    z = window(0)
    supply = window(1)
    high = z.shape[0]
    beside_z = {step: turn(z, step, 1) for step in (-1, 0, 1)}
    slopes = []
    for k, (step_row, step_col) in enumerate(OFFSETS):
        slopes.append(coef[k] * jnp.maximum(z - turn(beside_z[step_col], step_row, 0), 0.0))
    share = 1.0 / (functools.reduce(jnp.add, slopes) + RETENTION)
    weight = {}
    for k, (step_row, step_col) in enumerate(OFFSETS):
        weight[step_row, step_col] = turn(slopes[k] * share, -step_col, 1)
    flow = supply
    for _ in range(ITERS):
        moved = {step: turn(flow, -step, 1) for step in (-1, 0, 1)}
        sums = {}
        for step_row in (-1, 0, 1):
            sums[step_row] = functools.reduce(
                jnp.add, [weight[step_row, c] * moved[c] for c in (-1, 0, 1) if (step_row, c) in weight])
        flow = supply + sums[0] + turn(sums[1], -1, 0) + turn(sums[-1], 1, 0)

    for slot, sign in ((0, 1), (1, -1)):
        lines = [vrecv[slot, line_at[slot] + 8 * i:line_at[slot] + 8 * i + 8, :] for i in range(2)]
        own_at = 56 + 2 * crows - 24 if slot == 0 else 0
        if slot == 0:
            three = [tall[32 + 2 * crows:40 + 2 * crows, :], lines[0], lines[1]]
            at = rows + 8
        else:
            three = [lines[0], lines[1], tall[0:8, :]]
            at = 7

        def beside_line(x, step):
            moved = pltpu.roll(x, 1 if step < 0 else LANES - 1, 1)
            edge = pltpu.roll(moved, 1 if step < 0 else 7, 0)
            return jnp.where(lane == (0 if step < 0 else LANES - 1), edge, moved)

        near = [{0: x, -1: beside_line(x, -1), 1: beside_line(x, 1)} for x in three]
        total_slope = jnp.full((8, LANES), RETENTION, F32)
        for k, (off_row, off_col) in enumerate(OFFSETS):
            total_slope = total_slope + coef[k] * jnp.maximum(three[1] - near[1 + off_row][off_col], 0.0)
        line_share = 1.0 / total_slope
        line_share = jnp.where(jnp.logical_and(sub == 0, lane == 0), 0.0, line_share)
        line_share = jnp.where(jnp.logical_and(sub == far, lane == LANES - 1), 0.0, line_share)
        for j in range(blocks):
            for step, ref in by_column.items():
                ref[j, at:at + 1, :] = near[1][step][j:j + 1, :]
            recip[j, at:at + 1, :] = line_share[j:j + 1, :]

    for g in (0, groups - 1):
        settle(g, [leaving(g, j) for j in range(blocks)])

    for number, way in enumerate((1, -1)):
        for h in range(halves):
            target = pl.ds(8 + 64 * h + (0 if way == 1 else 7), 8, stride=8)
            source = pl.ds(8 + 64 * h + (-1 if way == 1 else 8), 8, stride=8)
            fields = []
            for j in range(blocks):
                from_z, scale = zp[j, source, :], recip[j, source, :]
                fields.append([
                    coef[OFFSETS.index((way, c))] * jnp.maximum(from_z - by_column[c][j, target, :], 0.0) * scale for c in (-1, 0, 1)])
            for j in range(blocks):
                inner_edge[number, j, 8 * h:8 * h + 8, :], outer_edge[number, j, 8 * h:8 * h + 8, :] = across(fields, j)

    def column(own, left, right):
        beside = jnp.where(sub < 2, pltpu.roll(left, 4, 0), pltpu.roll(right, 4, 0))
        return jnp.where(jnp.logical_and(sub >= 2, sub < 6), own, beside)

    side_tile = [srecv[k, crows:crows + 8, :] for k in range(8)]
    tall_tile = [vrecv[slot, tile_at[slot]:tile_at[slot] + 8, :] for slot in range(2)]
    tile = side[crows:crows + 8, :]
    below = column(tall_tile[0], side_tile[3], side_tile[1])
    above = column(tall_tile[1], side_tile[5], side_tile[7])
    ze = jnp.concatenate([column(tile, side_tile[4], side_tile[0]), jnp.where(lane < half, below, above)], axis=1)
    sub_e = lax.broadcasted_iota(jnp.int32, (8, 2 * LANES), 0)
    beside_e = {step: turn(ze, step, 1) for step in (-1, 0, 1)}
    flux = {}
    for k, (off_row, off_col) in enumerate(OFFSETS):
        flux[off_row, off_col] = coef[k] * jnp.maximum(ze - turn(beside_e[off_row], off_col, 0), 0.0)
    share_e = 1.0 / (functools.reduce(jnp.add, flux.values()) + RETENTION)

    def lines_of(off_row):
        right, left = flux[off_row, 1] * share_e, flux[off_row, -1] * share_e
        picked = jnp.where(sub_e == 1, right, jnp.where(sub_e == 6, left, 0.0))
        picked = jnp.where(sub_e == 3, pltpu.roll(right, 1, 0), jnp.where(sub_e == 4, pltpu.roll(left, 7, 0), picked))
        if off_row == 0:
            return picked
        return jnp.where(jnp.logical_or(sub_e == 2, sub_e == 5), flux[off_row, 0] * share_e, picked)

    from_above = turn(lines_of(1), -1, 1)[:, :LANES]
    from_below = turn(lines_of(-1), 1, 1)[:, :LANES]
    inside = lines_of(0)[:, :LANES] + jnp.where(first, 0.0, from_above) + jnp.where(last, 0.0, from_below)
    outside = jnp.where(first, from_above, jnp.where(last, from_below, 0.0))
    gap = jnp.zeros((LANES - 16, LANES), F32)

    def upright(lines, width):
        if width == 2:
            top = jnp.where(sub < 2, pltpu.roll(lines, 6, 0), 0.0)
            bottom = jnp.where(sub >= 6, pltpu.roll(lines, 2, 0), 0.0)
        else:
            top = jnp.where(sub == 0, pltpu.roll(lines, 7, 0), 0.0)
            bottom = jnp.where(sub == 7, pltpu.roll(lines, 1, 0), 0.0)
        return jnp.transpose(jnp.concatenate([top, gap, bottom], axis=0))

    for field, width in ((inner, 2), (outer, 1)):
        values = upright(inside, width)
        for g in range(groups):
            at = slice(8 * g, 8 * g + 8)
            field[0, at, :] = field[0, at, :] + jnp.where(lane < half, values[at], 0.0)
            field[far, at, :] = field[far, at, :] + jnp.where(lane < half, 0.0, values[at])
    for field, width in ((inner_edge, 2), (outer_edge, 1)):
        turned[width - 1] = upright(outside, width)
        for number in range(2):
            for h in range(halves):
                at = slice(8 * h, 8 * h + 8)
                values = turned[width - 1, pl.ds(64 * h + 7 * number, 8, stride=8), :]
                field[number, 0, at, :] = field[number, 0, at, :] + jnp.where(lane < half, values, 0.0)
                field[number, far, at, :] = field[number, far, at, :] + jnp.where(lane < half, 0.0, values)

    left = turn(flow, -1, 1)[:, :LANES]
    right = turn(flow, 1, 1)[:, :LANES]
    centre = flow[:, :LANES]
    per_block = LANES // 8
    for j in range(blocks):
        index = lane // 8 + j * per_block
        spread = []
        for at in list(range(0, crows, 8)) + [crows, high - 8]:
            mid = take_lanes(centre[at:at + 8], index)
            beside = jnp.where(first, take_lanes(left[at:at + 8], index), take_lanes(right[at:at + 8], index))
            spread.append((mid, beside))
        for h in range(halves):
            for number in range(2):
                terms = []
                for which in range(2):
                    here = spread[h][which]
                    if number == 0:
                        other = spread[h - 1][which] if h > 0 else spread[-1][which]
                        level = jnp.where(sub == 0, pltpu.roll(other, 1, 0), pltpu.roll(here, 1, 0))
                    else:
                        other = spread[h + 1][which] if h < halves - 1 else spread[-2][which]
                        level = jnp.where(sub == 7, pltpu.roll(other, 7, 0), pltpu.roll(here, 7, 0))
                    terms.append((inner_edge, outer_edge)[which][number, j, 8 * h:8 * h + 8, :] * level)
                at = pl.ds(64 * h + 7 * number, 8, stride=8)
                base[j, at, :] = base[j, at, :] + (terms[0] + terms[1])
        for g in range(groups):
            def level(number):
                return jnp.broadcast_to(spread[g // 8][number][g % 8:g % 8 + 1, :], (8, LANES))

            at = slice(8 * g, 8 * g + 8)
            out_ref[at, j * LANES:(j + 1) * LANES] = base[j, at, :] + inner[j, at, :] * level(0) + outer[j, at, :] * level(1)

    for k in range(8):
        @pl.when(exists[k])
        def _():
            copies(k).wait_send()


def solution(mesh):
    row_devices, col_devices = mesh.shape["rows"], mesh.shape["cols"]

    def on_device(elevation, data_mask, tie_order):
        rows, cols = elevation.shape
        groups, blocks = rows // 8, cols // LANES
        tall = 24 + 2 * groups
        return pl.pallas_call(
            functools.partial(kernel, row_devices, col_devices),
            out_shape=pltpu.VMEM((rows, cols), F32),
            in_specs=[pl.BlockSpec(memory_space=pl.ANY)] * 3,
            out_specs=pl.BlockSpec(memory_space=pltpu.VMEM),
            scratch_shapes=[
                pltpu.SMEM((8,), jnp.int32),
                pltpu.VMEM((blocks, rows + 16, LANES), F32),
                pltpu.VMEM((blocks, rows + 16, LANES), F32),
                pltpu.VMEM((blocks, rows + 16, LANES), F32),
                pltpu.VMEM((blocks, rows, LANES), jnp.int32),
                pltpu.VMEM((blocks, rows + 16, LANES), F32),
                pltpu.VMEM((blocks, 3, 8, LANES), F32),
                pltpu.VMEM((blocks, rows, LANES), F32),
                pltpu.VMEM((blocks, rows, LANES), F32),
                pltpu.VMEM((blocks, rows, LANES), F32),
                pltpu.VMEM((2, blocks, groups, LANES), F32),
                pltpu.VMEM((2, blocks, groups, LANES), F32),
                pltpu.VMEM((2, rows, LANES), F32),
                pltpu.VMEM((cols, LANES), jnp.bfloat16),
                pltpu.VMEM((groups + 8, LANES), F32),
                pltpu.VMEM((tall + 16, LANES), F32),
                pltpu.VMEM((8, groups + 8, LANES), F32),
                pltpu.VMEM((2, tall, LANES), F32),
                pltpu.SemaphoreType.DMA((2 * blocks,)),
                pltpu.SemaphoreType.DMA,
                pltpu.SemaphoreType.DMA((8,)),
                pltpu.SemaphoreType.DMA((8,)),
            ],
            compiler_params=pltpu.CompilerParams(collective_id=0, has_side_effects=True, vmem_limit_bytes=61000000),
        )(tie_order, elevation, data_mask)

    return jax.shard_map(
        on_device, mesh=mesh, in_specs=(P("rows", "cols"), P("rows", "cols"), P()),
        out_specs=P("rows", "cols"), check_vma=False)
```

time: 14.1 us -> 9.38 us (0.67)
  the two profiles are of different devices: /device:TPU:1 before, /device:TPU:0 now
where the time goes in v1:
time: 9.38 us; the launch traced here: 9.21 us
  Pallas kernels  8.41 us (90%)
  local copies, waits for them, and re-layouts  0.8 us (9%)
    pallas_call x1, Pallas kernels, on_device(): pl.pallas_call(functools.partial(kernel, row_devices, col_devices), out_s...  8.41 us
    unnamed x1, local copies, waits for them, and re-layouts  0.8 us

profile of v1, /device:TPU:0, one launch (start us, length us, event | category | flops | bytes accessed | tf_op | source)
XLA Modules:
  0.0 9.2 jit_solution(2796871485096418620)
XLA Ops:
  0.0 8.4 %shard_map.37 = f32[128,1024]{1,0:T(8,128)S(1)} custom-call(s32[8]{0:T(128)} %tie_hbm.1, f32[128,1024]{1,0:T(8,128)} %elev_ref.1, s32[128,1024]{1,0:T(8,128)} %mask_ref.1), custom_call_target="tpu_custom_call" | custom-call | tf_op jit(solution)/shard_map/pallas_call | solution.py:415
  8.4 0.8 %copy.5 = f32[128,1024]{1,0:T(8,128)} copy(f32[128,1024]{1,0:T(8,128)S(1)} %shard_map.37) | data formatting | bytes 1048576

commit v2 on v1

--- a/solution.py
+++ b/solution.py
@@ -39,8 +39,8 @@
     return jnp.take_along_axis(values, index, axis=1, mode="promise_in_bounds")
 
 
-def kernel(row_devices, col_devices, tie_hbm, elev_ref, mask_ref, out_ref, tie_ref, zp, zl, zr, mask, recip, pending, base, inner, outer,
-           inner_edge, outer_edge, turned, ones, side, tall, srecv, vrecv, load_sem, tie_sem, send_sem, recv_sem):
+def kernel(row_devices, col_devices, tie_hbm, elev_ref, mask_ref, out_ref, tie_ref, zp, zl, zr, mask, recip, base, inner, outer,
+           inner_edge, outer_edge, turned, ones, sums, side, tall, srecv, vrecv, load_sem, tie_sem, send_sem, recv_sem):
     rows, cols = elev_ref.shape
     groups, blocks = rows // 8, cols // LANES
     crows, halves = groups, groups // 8
@@ -82,8 +82,6 @@
 
     lane = lax.broadcasted_iota(jnp.int32, (8, LANES), 1)
     sub = lax.broadcasted_iota(jnp.int32, (8, LANES), 0)
-    lane_c = lax.broadcasted_iota(jnp.int32, (crows, LANES), 1)
-    middle_lanes = jnp.logical_and(lane_c >= LANES // 4, lane_c < 3 * LANES // 4)
     first, last = (lane & 7) == 0, (lane & 7) == 7
     half = LANES // 2
     nothing = jnp.zeros((8, LANES), F32)
@@ -94,41 +92,59 @@
         lax.broadcasted_iota(jnp.int32, (cols, LANES), 0) // 8 == lax.broadcasted_iota(jnp.int32, (cols, LANES), 1)
     ).astype(F32).astype(jnp.bfloat16)
 
-    loads[0][0].wait()
-    loads[far][0].wait()
-    ends = jnp.where(lax.broadcasted_iota(jnp.int32, (rows, LANES), 1) < half, zp[0, 8:8 + rows, :], zp[far, 8:8 + rows, :])
-    ends = jnp.transpose(ends)
-    tile = jnp.where(sub < 4, pltpu.roll(ends[0:8], 2, 0), pltpu.roll(ends[LANES - 8:LANES], 6, 0))
-    side[crows:crows + 8, :] = tile
-    tall[16 + 2 * crows:24 + 2 * crows, :] = tile
-
-    total = jnp.zeros((4 * crows, LANES), F32)
-    for j in loads:
-        if j not in (0, far):
+    order = list(loads)
+
+    def row_sums(some):
+        for j in some:
+            height_sum = jnp.zeros((crows, LANES), F32)
+            count_sum = jnp.zeros((crows, LANES), F32)
+            for s in range(8):
+                valid = mask[j, pl.ds(s, crows, stride=8), :].astype(F32)
+                height_sum = height_sum + valid * zp[j, pl.ds(8 + s, crows, stride=8), :]
+                count_sum = count_sum + valid
+            high = height_sum.astype(jnp.bfloat16)
+            rest = height_sum - high.astype(F32)
+            middle = rest.astype(jnp.bfloat16)
+            low = (rest - middle.astype(F32)).astype(jnp.bfloat16)
+            sums[:, j * LANES:(j + 1) * LANES] = jnp.concatenate([count_sum.astype(jnp.bfloat16), high, middle, low], axis=0)
+            for number, at in enumerate((8, 9, rows + 6, rows + 7)):
+                line = (0, 8, 24 + 2 * crows, 32 + 2 * crows)[number]
+                tall[line + j:line + j + 1, :] = zp[j, at:at + 1, :]
+
+    for part in (order[:blocks // 2], order[blocks // 2:]):
+        for j in part:
             loads[j][0].wait()
-        loads[j][1].wait()
-        height_sum = jnp.zeros((crows, LANES), F32)
-        count_sum = jnp.zeros((crows, LANES), F32)
-        for s in range(8):
-            valid = mask[j, pl.ds(s, crows, stride=8), :].astype(F32)
-            height_sum = height_sum + valid * zp[j, pl.ds(8 + s, crows, stride=8), :]
-            count_sum = count_sum + valid
-        high = height_sum.astype(jnp.bfloat16)
-        rest = height_sum - high.astype(F32)
-        middle = rest.astype(jnp.bfloat16)
-        low = (rest - middle.astype(F32)).astype(jnp.bfloat16)
-        stacked = jnp.concatenate([count_sum.astype(jnp.bfloat16), high, middle, low], axis=0)
-        total = total + jnp.dot(stacked, ones[j * LANES:(j + 1) * LANES, :], preferred_element_type=F32)
-        for number, at in enumerate((8, 9, rows + 6, rows + 7)):
-            line = (0, 8, 24 + 2 * crows, 32 + 2 * crows)[number]
-            tall[line + j:line + j + 1, :] = zp[j, at:at + 1, :]
+            loads[j][1].wait()
+        if 0 in part:
+            ends = jnp.where(lax.broadcasted_iota(jnp.int32, (rows, LANES), 1) < half, zp[0, 8:8 + rows, :], zp[far, 8:8 + rows, :])
+            ends = jnp.transpose(ends)
+            tile = jnp.where(sub < 4, pltpu.roll(ends[0:8], 2, 0), pltpu.roll(ends[LANES - 8:LANES], 6, 0))
+            tall[16 + 2 * crows:24 + 2 * crows, :] = tile
+        row_sums(part)
+    total = jnp.dot(sums[...], ones[...], preferred_element_type=F32)
     counts = total[0:crows]
     heights = total[crows:2 * crows] + (total[2 * crows:3 * crows] + total[3 * crows:])
     overview = heights / (counts + 1.0)
     runoff = counts * (1.0 / 64.0)
-    side[0:crows, :] = jnp.where(middle_lanes, pltpu.roll(runoff, half, 1), overview)
     tall[16:16 + crows, :] = overview
     tall[16 + crows:16 + 2 * crows, :] = runoff
+
+    quarter, place = lane // 32, lane & 15
+    early = (lane & 31) < 16
+    eastward, westward = [], []
+    for h in range(halves):
+        at = slice(8 * h, 8 * h + 8)
+        height = take_lanes(overview[at], jnp.where(early, LANES - 16, 0) + place)
+        count = take_lanes(runoff[at], jnp.where(early, 0, LANES - 16) + place)
+        for whole, value in ((eastward, jnp.where(early, height, count)), (westward, jnp.where(early, count, height))):
+            whole += [value, pltpu.roll(value, 4, 0)]
+
+    def quarters(whole):
+        return jnp.where(quarter < 2, jnp.where(quarter == 0, whole[0], whole[1]), jnp.where(quarter == 2, whole[2], whole[3]))
+
+    tile = tall[16 + 2 * crows:24 + 2 * crows, :]
+    side[0] = jnp.where(sub < 4, quarters(eastward), tile)
+    side[1] = jnp.where(sub < 4, tile, quarters(westward))
 
     pl.semaphore_wait(barrier, functools.reduce(jnp.add, [there.astype(jnp.int32) for there in exists]))
 
@@ -137,7 +153,7 @@
         if k in UPDOWN:
             src, dst = tall.at[pl.ds(16 if k == 2 else 0, 24 + 2 * crows), :], vrecv.at[slot // 4]
         else:
-            src, dst = side, srecv.at[slot]
+            src, dst = side.at[0 if OFFSETS[k][1] > 0 else 1], srecv.at[slot]
         return pltpu.make_async_remote_copy(
             src_ref=src, dst_ref=dst, send_sem=send_sem.at[k], recv_sem=recv_sem.at[slot],
             device_id=peer(k), device_id_type=pl.DeviceIdType.MESH)
@@ -155,8 +171,8 @@
                     start = 16 + crows if k == 2 else crows
                     vrecv[k // 4, at:at + 8, :] = jnp.full((8, LANES), 0.0 if start <= at < start + crows else OUTSIDE, F32)
             else:
-                srecv[k, 0:crows, :] = jnp.where(middle_lanes, 0.0, OUTSIDE)
-                srecv[k, crows:crows + 8, :] = jnp.full((8, LANES), OUTSIDE, F32)
+                empty = jnp.logical_and(early, sub >= 4) if OFFSETS[k][1] > 0 else jnp.logical_and(jnp.logical_not(early), sub < 4)
+                srecv[k] = jnp.where(empty, 0.0, OUTSIDE)
 
     tie_load.wait()
     coef = coefficients(tie_ref)
@@ -206,18 +222,8 @@
         for j in range(blocks):
             inner[j, pl.ds(8 * g, 8), :], outer[j, pl.ds(8 * g, 8), :] = across(fields, j)
 
-    pending[...] = jnp.zeros(pending.shape, F32)
-
-    def step(g, carry):
-        fields = [[pending[j, c] for c in range(3)] for j in range(blocks)]
-        settle(g - 1, fields)
-        for j in range(blocks):
-            for c, value in enumerate(leaving(g, j)):
-                pending[j, c] = value
-        return carry
-
-    lax.fori_loop(1, groups - 1, step, 0)
-    settle(groups - 2, [[pending[j, c] for c in range(3)] for j in range(blocks)])
+    for g in range(1, groups - 1):
+        settle(g, [leaving(g, j) for j in range(blocks)])
 
     for k in range(8):
         @pl.when(exists[k])
@@ -232,9 +238,19 @@
     line_at = (0, 24 + 2 * crows - 16)
 
     def window(field):
+        def unpacked(k, h):
+            given = srecv[k]
+            swapped = pltpu.roll(given, 4, 0)
+            if OFFSETS[k][1] > 0:
+                start, first_rows, last_rows = 16 * (1 - field), swapped, given
+            else:
+                start, first_rows, last_rows = 16 * field + 16, given, swapped
+            return jnp.where(
+                sub < 4, turn(first_rows, start + 64 * h + (32 if OFFSETS[k][1] > 0 else 0), 1),
+                turn(last_rows, start + 64 * h + (0 if OFFSETS[k][1] > 0 else 32), 1))
+
         def beside(right, left):
-            a, b = srecv[right, 0:crows, :], srecv[left, 0:crows, :]
-            return jnp.where(lane_c < half, a, b) if field == 0 else pltpu.roll(jnp.where(lane_c < half, b, a), half, 1)
+            return jnp.concatenate([jnp.where(lane < half, unpacked(right, h), unpacked(left, h)) for h in range(halves)], axis=0)
 
         def level(slot):
             return vrecv[slot, coarse_at[slot] + field * crows:coarse_at[slot] + (field + 1) * crows, :]
@@ -245,10 +261,6 @@
         sub_w = lax.broadcasted_iota(jnp.int32, (8, 2 * LANES), 0)
         mixed = jnp.where(sub_w < 4, below[8:16], above[crows - 16:crows - 8])
         return jnp.concatenate([here, below[0:8], mixed, above[crows - 8:crows]], axis=0)
-
-    def shares(z):
-        beside_rows = {step: turn(z, step, 1) for step in (-1, 0, 1)}
-        return beside_rows
 
     z = window(0)
     supply = window(1)
@@ -272,7 +284,6 @@
 
     for slot, sign in ((0, 1), (1, -1)):
         lines = [vrecv[slot, line_at[slot] + 8 * i:line_at[slot] + 8 * i + 8, :] for i in range(2)]
-        own_at = 56 + 2 * crows - 24 if slot == 0 else 0
         if slot == 0:
             three = [tall[32 + 2 * crows:40 + 2 * crows, :], lines[0], lines[1]]
             at = rows + 8
@@ -316,9 +327,9 @@
         beside = jnp.where(sub < 2, pltpu.roll(left, 4, 0), pltpu.roll(right, 4, 0))
         return jnp.where(jnp.logical_and(sub >= 2, sub < 6), own, beside)
 
-    side_tile = [srecv[k, crows:crows + 8, :] for k in range(8)]
+    side_tile = [srecv[k] for k in range(8)]
     tall_tile = [vrecv[slot, tile_at[slot]:tile_at[slot] + 8, :] for slot in range(2)]
-    tile = side[crows:crows + 8, :]
+    tile = tall[16 + 2 * crows:24 + 2 * crows, :]
     below = column(tall_tile[0], side_tile[3], side_tile[1])
     above = column(tall_tile[1], side_tile[5], side_tile[7])
     ze = jnp.concatenate([column(tile, side_tile[4], side_tile[0]), jnp.where(lane < half, below, above)], axis=1)
@@ -424,7 +435,6 @@
                 pltpu.VMEM((blocks, rows + 16, LANES), F32),
                 pltpu.VMEM((blocks, rows, LANES), jnp.int32),
                 pltpu.VMEM((blocks, rows + 16, LANES), F32),
-                pltpu.VMEM((blocks, 3, 8, LANES), F32),
                 pltpu.VMEM((blocks, rows, LANES), F32),
                 pltpu.VMEM((blocks, rows, LANES), F32),
                 pltpu.VMEM((blocks, rows, LANES), F32),
@@ -432,9 +442,10 @@
                 pltpu.VMEM((2, blocks, groups, LANES), F32),
                 pltpu.VMEM((2, rows, LANES), F32),
                 pltpu.VMEM((cols, LANES), jnp.bfloat16),
-                pltpu.VMEM((groups + 8, LANES), F32),
+                pltpu.VMEM((4 * groups, cols), jnp.bfloat16),
+                pltpu.VMEM((2, 8, LANES), F32),
                 pltpu.VMEM((tall + 16, LANES), F32),
-                pltpu.VMEM((8, groups + 8, LANES), F32),
+                pltpu.VMEM((8, 8, LANES), F32),
                 pltpu.VMEM((2, tall, LANES), F32),
                 pltpu.SemaphoreType.DMA((2 * blocks,)),
                 pltpu.SemaphoreType.DMA,

time: 9.38 us -> 9.34 us (level)
  no operation moved by 1% of the time
where the time goes in v2:
time: 9.34 us; the launch traced here: 9.17 us
  Pallas kernels  8.37 us (90%)
  local copies, waits for them, and re-layouts  0.8 us (9%)
    pallas_call x1, Pallas kernels, on_device(): pl.pallas_call(functools.partial(kernel, row_devices, col_devices), out_s...  8.37 us
    unnamed x1, local copies, waits for them, and re-layouts  0.8 us

profile of v2, /device:TPU:0, one launch (start us, length us, event | category | flops | bytes accessed | tf_op | source)
XLA Modules:
  0.0 9.2 jit_solution(8284523979751869397)
XLA Ops:
  0.0 8.4 %shard_map.37 = f32[128,1024]{1,0:T(8,128)S(1)} custom-call(s32[8]{0:T(128)} %tie_hbm.1, f32[128,1024]{1,0:T(8,128)} %elev_ref.1, s32[128,1024]{1,0:T(8,128)} %mask_ref.1), custom_call_target="tpu_custom_call" | custom-call | tf_op jit(solution)/shard_map/pallas_call | solution.py:426
  8.4 0.8 %copy.5 = f32[128,1024]{1,0:T(8,128)} copy(f32[128,1024]{1,0:T(8,128)S(1)} %shard_map.37) | data formatting | bytes 1048576

commit v3 on v2

v3 whole, which is shorter than its diff:
```python
import functools

import jax
import jax.numpy as jnp
from jax import lax
from jax.experimental import pallas as pl
from jax.experimental.pallas import tpu as pltpu
from jax.sharding import PartitionSpec as P

ITERS = 8
OFFSETS = ((0, 1), (1, 1), (1, 0), (1, -1), (0, -1), (-1, -1), (-1, 0), (-1, 1))
RECIPROCAL = (1.0, 0.7071067811865476) * 4
RETENTION = 0.1
OUTSIDE = 1000.0
LANES = 128
F32 = jnp.float32


def coefficients(tie_ref):
    out = []
    for k in range(8):
        value = jnp.float32(0.0)
        for i in range(8):
            place = jnp.float32((1.0 + 0.5 * (7.0 - i) / 7.0) * RECIPROCAL[k])
            value = jnp.where(tie_ref[i] == k, place, value)
        out.append(value)
    return out


def shift_lanes(before, here, after, step, lane):
    if step == 0:
        return here
    if step < 0:
        return pltpu.roll(jnp.where(lane == LANES - 1, before, here), 1, 1)
    return pltpu.roll(jnp.where(lane == 0, after, here), LANES - 1, 1)


def take_lanes(values, index):
    return jnp.take_along_axis(values, index, axis=1, mode="promise_in_bounds")


def exchange(row_devices, col_devices, tie_hbm, elev_ref, mask_ref, flow_ref, base, inner, outer, inner_edge, outer_edge,
             tie_ref, zp, zl, zr, mask, recip, turned, ones, sums, side, tall, srecv, vrecv, load_sem, tie_sem, send_sem, recv_sem):
    rows, cols = elev_ref.shape
    groups, blocks = rows // 8, cols // LANES
    crows, halves = groups, groups // 8
    row, col = lax.axis_index("rows"), lax.axis_index("cols")
    far = blocks - 1

    loads = {}
    for j in [0, far] + list(range(1, far)):
        part = pl.ds(j * LANES, LANES)
        loads[j] = (
            pltpu.make_async_copy(elev_ref.at[:, part], zp.at[j, pl.ds(8, rows), :], load_sem.at[j]),
            pltpu.make_async_copy(mask_ref.at[:, part], mask.at[j], load_sem.at[blocks + j]))
        loads[j][0].start()
        loads[j][1].start()
    tie_load = pltpu.make_async_copy(tie_hbm, tie_ref, tie_sem)
    tie_load.start()

    barrier = pltpu.get_barrier_semaphore()
    exists = []
    for step_row, step_col in OFFSETS:
        there = jnp.bool_(True)
        if step_row > 0:
            there = row < row_devices - 1
        if step_row < 0:
            there = row > 0
        if step_col > 0:
            there = jnp.logical_and(there, col < col_devices - 1)
        if step_col < 0:
            there = jnp.logical_and(there, col > 0)
        exists.append(there)

    def peer(k):
        return {"rows": row + OFFSETS[k][0], "cols": col + OFFSETS[k][1]}

    for k in range(8):
        @pl.when(exists[k])
        def _():
            pl.semaphore_signal(barrier, inc=1, device_id=peer(k), device_id_type=pl.DeviceIdType.MESH)

    lane = lax.broadcasted_iota(jnp.int32, (8, LANES), 1)
    sub = lax.broadcasted_iota(jnp.int32, (8, LANES), 0)
    first, last = (lane & 7) == 0, (lane & 7) == 7
    lane_c = lax.broadcasted_iota(jnp.int32, (crows, LANES), 1)
    middle_lanes = jnp.logical_and(lane_c >= LANES // 4, lane_c < 3 * LANES // 4)
    half = LANES // 2
    nothing = jnp.zeros((8, LANES), F32)

    SIDES, UPDOWN = (0, 1, 3, 4, 5, 7), (2, 6)

    taker = lax.broadcasted_iota(jnp.int32, (cols, LANES), 1)
    giver = lax.broadcasted_iota(jnp.int32, (cols, LANES), 0) // 8
    ones[:, :LANES] = (giver == taker).astype(F32).astype(jnp.bfloat16)
    ones[:, LANES:] = (giver == (taker ^ half)).astype(F32).astype(jnp.bfloat16)

    order = list(loads)

    def row_sums(some):
        for j in some:
            height_sum = jnp.zeros((crows, LANES), F32)
            count_sum = jnp.zeros((crows, LANES), F32)
            for s in range(8):
                valid = mask[j, pl.ds(s, crows, stride=8), :].astype(F32)
                height_sum = height_sum + valid * zp[j, pl.ds(8 + s, crows, stride=8), :]
                count_sum = count_sum + valid
            high = height_sum.astype(jnp.bfloat16)
            rest = height_sum - high.astype(F32)
            middle = rest.astype(jnp.bfloat16)
            low = (rest - middle.astype(F32)).astype(jnp.bfloat16)
            sums[:, j * LANES:(j + 1) * LANES] = jnp.concatenate([count_sum.astype(jnp.bfloat16), high, middle, low], axis=0)
            for number, at in enumerate((8, 9, rows + 6, rows + 7)):
                line = (0, 8, 24 + 2 * crows, 32 + 2 * crows)[number]
                tall[line + j:line + j + 1, :] = zp[j, at:at + 1, :]

    for part in [order[at:at + 2] for at in range(0, blocks, 2)]:
        for j in part:
            loads[j][0].wait()
            loads[j][1].wait()
        if 0 in part:
            ends = jnp.where(lax.broadcasted_iota(jnp.int32, (rows, LANES), 1) < half, zp[0, 8:8 + rows, :], zp[far, 8:8 + rows, :])
            ends = jnp.transpose(ends)
            tile = jnp.where(sub < 4, pltpu.roll(ends[0:8], 2, 0), pltpu.roll(ends[LANES - 8:LANES], 6, 0))
            tall[16 + 2 * crows:24 + 2 * crows, :] = tile
            side[crows:crows + 8, :] = tile
        row_sums(part)
    both = jnp.dot(sums[...], ones[...], preferred_element_type=F32)
    total = both[:, :LANES]
    counts = total[0:crows]
    heights = total[crows:2 * crows] + (total[2 * crows:3 * crows] + total[3 * crows:])
    overview = heights / (counts + 1.0)
    runoff = counts * (1.0 / 64.0)
    tall[16:16 + crows, :] = overview
    tall[16 + crows:16 + 2 * crows, :] = runoff

    side[0:crows, :] = jnp.where(middle_lanes, both[0:crows, LANES:] * (1.0 / 64.0), overview)

    pl.semaphore_wait(barrier, functools.reduce(jnp.add, [there.astype(jnp.int32) for there in exists]))

    def copies(k, arriving=False):
        slot = k if arriving else (k + 4) % 8
        if k in UPDOWN:
            src, dst = tall.at[pl.ds(16 if k == 2 else 0, 24 + 2 * crows), :], vrecv.at[slot // 4]
        else:
            src, dst = side, srecv.at[slot]
        return pltpu.make_async_remote_copy(
            src_ref=src, dst_ref=dst, send_sem=send_sem.at[k], recv_sem=recv_sem.at[slot],
            device_id=peer(k), device_id_type=pl.DeviceIdType.MESH)

    for k in (5, 4, 6, 7, 3, 1, 0, 2):
        @pl.when(exists[k])
        def _():
            copies(k).start()

    for k in range(8):
        @pl.when(jnp.logical_not(exists[k]))
        def _():
            if k in UPDOWN:
                for at in range(0, 24 + 2 * crows, 8):
                    start = 16 + crows if k == 2 else crows
                    vrecv[k // 4, at:at + 8, :] = jnp.full((8, LANES), 0.0 if start <= at < start + crows else OUTSIDE, F32)
            else:
                srecv[k, 0:crows, :] = jnp.where(middle_lanes, 0.0, OUTSIDE)
                srecv[k, crows:crows + 8, :] = jnp.full((8, LANES), OUTSIDE, F32)

    tie_load.wait()
    coef = coefficients(tie_ref)

    for ref in (zp, zl, zr, recip):
        for j in range(blocks):
            ref[j, 0:8, :], ref[j, 8 + rows:16 + rows, :] = nothing, nothing

    for g in range(groups):
        at = pl.ds(8 * g + 8, 8)
        for j in range(blocks):
            here = zp[j, at, :]
            before, after = zp[(j - 1) % blocks, at, :], zp[(j + 1) % blocks, at, :]
            zl[j, at, :] = shift_lanes(before, here, after, -1, lane)
            zr[j, at, :] = shift_lanes(before, here, after, 1, lane)
            base[j, pl.ds(8 * g, 8), :] = mask[j, pl.ds(8 * g, 8), :].astype(F32)

    by_column = {-1: zl, 0: zp, 1: zr}

    def within(j, share):
        if j == 0:
            share = jnp.where(lane == 0, 0.0, share)
        if j == far:
            share = jnp.where(lane == LANES - 1, 0.0, share)
        return share

    def leaving(g, j):
        here = zp[j, pl.ds(8 * g + 8, 8), :]
        slopes = {}
        for k, (off_row, off_col) in enumerate(OFFSETS):
            beside = by_column[off_col][j, pl.ds(8 * g + 8 + off_row, 8), :]
            slopes[off_row, off_col] = coef[k] * jnp.maximum(here - beside, 0.0)
        share = within(j, 1.0 / (functools.reduce(jnp.add, slopes.values()) + RETENTION))
        if g == 0:
            share = jnp.where(sub == 0, 0.0, share)
        if g == groups - 1:
            share = jnp.where(sub == 7, 0.0, share)
        recip[j, pl.ds(8 * g + 8, 8), :] = share
        down, up = jnp.where(sub == 7, 0.0, share), jnp.where(sub == 0, 0.0, share)
        out = []
        for c in (-1, 0, 1):
            moved = pltpu.roll(slopes[1, c] * down, 1, 0) + pltpu.roll(slopes[-1, c] * up, 7, 0)
            out.append(moved if c == 0 else moved + slopes[0, c] * share)
        return out

    def across(fields, j):
        west = fields[j - 1][2] if j > 0 else nothing
        east = fields[j + 1][0] if j < far else nothing
        from_west = pltpu.roll(jnp.where(lane == LANES - 1, west, fields[j][2]), 1, 1)
        from_east = pltpu.roll(jnp.where(lane == 0, east, fields[j][0]), LANES - 1, 1)
        kept = fields[j][1] + jnp.where(first, 0.0, from_west) + jnp.where(last, 0.0, from_east)
        return kept, jnp.where(first, from_west, jnp.where(last, from_east, 0.0))

    def settle(g, fields):
        for j in range(blocks):
            at = pl.ds(j * rows + 8 * g, 8)
            inner[at, :], outer[at, :] = across(fields, j)

    for g in range(groups):
        settle(g, [leaving(g, j) for j in range(blocks)])

    def edge_at(number, j, h):
        return pl.ds((number * blocks + j) * groups + 8 * h, 8)

    def compact(number, way, h):
        target = pl.ds(8 + 64 * h + (0 if way == 1 else 7), 8, stride=8)
        source = pl.ds(8 + 64 * h + (-1 if way == 1 else 8), 8, stride=8)
        fields = []
        for j in range(blocks):
            from_z, scale = zp[j, source, :], recip[j, source, :]
            fields.append([
                coef[OFFSETS.index((way, c))] * jnp.maximum(from_z - by_column[c][j, target, :], 0.0) * scale for c in (-1, 0, 1)])
        for j in range(blocks):
            at = edge_at(number, j, h)
            inner_edge[at, :], outer_edge[at, :] = across(fields, j)

    for number, way in enumerate((1, -1)):
        for h in range(halves):
            compact(number, way, h)

    for k in range(8):
        @pl.when(exists[k])
        def _():
            copies(k, arriving=True).wait_recv()

    def turn(x, step, axis):
        return x if step == 0 else pltpu.roll(x, (-step) % x.shape[axis], axis)

    coarse_at = (16, 0)
    tile_at = (16 + 2 * crows, 2 * crows)
    line_at = (0, 24 + 2 * crows - 16)

    def stacked(of_place):
        end = halves - 1
        rows_of = [of_place(None, h) for h in range(halves)] + [of_place(0, 0)]
        return jnp.concatenate(rows_of + [jnp.where(sub < 4, of_place(0, 1), of_place(1, end - 1)), of_place(1, end)], axis=0)

    def middle_of(field):
        def of_place(slot, h):
            if slot is None:
                return tall[16 + field * crows + 8 * h:24 + field * crows + 8 * h, :]
            return vrecv[slot, coarse_at[slot] + field * crows + 8 * h:coarse_at[slot] + field * crows + 8 * h + 8, :]

        return stacked(of_place)

    def beside_of(east):
        ks = {None: 0 if east else 4, 0: 1 if east else 3, 1: 7 if east else 5}
        return stacked(lambda slot, h: srecv[ks[slot], 8 * h:8 * h + 8, :])

    east, west = beside_of(True), beside_of(False)
    nearer = lax.broadcasted_iota(jnp.int32, east.shape, 1) < half
    z = jnp.concatenate([middle_of(0), jnp.where(nearer, east, west)], axis=1)
    supply = jnp.concatenate([middle_of(1), pltpu.roll(jnp.where(nearer, west, east), half, 1)], axis=1)
    beside_z = {step: turn(z, step, 1) for step in (-1, 0, 1)}
    slopes = []
    for k, (step_row, step_col) in enumerate(OFFSETS):
        slopes.append(coef[k] * jnp.maximum(beside_z[0] - turn(beside_z[step_col], step_row, 0), 0.0))
    share = 1.0 / (functools.reduce(jnp.add, slopes) + RETENTION)

    def core(x):
        return jnp.concatenate([x[0:crows + 8], x[crows + 16:]], axis=0)

    weight = {}
    given = {-1: 0.0, 0: 0.0, 1: 0.0}
    for k, (step_row, step_col) in enumerate(OFFSETS):
        source = slopes[k] * share
        given[step_col] = given[step_col] + turn(source * supply, -step_row, 0)
        weight[step_row, step_col] = source
    flow = core(supply + given[0] + turn(given[1], -1, 1) + turn(given[-1], 1, 1))
    weight = {at: turn(core(weight[at]), -at[1], 1) for at in weight}
    supply = core(supply)

    def sweep(flow):
        moved = {step: turn(flow, -step, 1) for step in (-1, 0, 1)}
        sums = {}
        for step_row in (-1, 0, 1):
            sums[step_row] = functools.reduce(
                jnp.add, [weight[step_row, c] * moved[c] for c in (-1, 0, 1) if (step_row, c) in weight])
        return supply + sums[0] + turn(sums[1], -1, 0) + turn(sums[-1], 1, 0)

    def beside_line(x, step):
        moved = pltpu.roll(x, 1 if step < 0 else LANES - 1, 1)
        edge = pltpu.roll(moved, 1 if step < 0 else 7, 0)
        return jnp.where(lane == (0 if step < 0 else LANES - 1), edge, moved)

    def around(line):
        return {0: line, -1: beside_line(line, -1), 1: beside_line(line, 1)}

    outermost = jnp.logical_or(jnp.logical_and(sub == 0, lane == 0), jnp.logical_and(sub == far, lane == LANES - 1))
    own_lines = ([32 + 2 * crows, 24 + 2 * crows], [0, 8])
    own_lines = [[around(tall[at:at + 8, :]) for at in pair] for pair in own_lines]

    def edge_row(slot):
        inward, number = (-1, 1) if slot == 0 else (1, 0)
        outside = [around(vrecv[slot, line_at[slot] + 8 * i:line_at[slot] + 8 * i + 8, :]) for i in ((0, 1) if slot == 0 else (1, 0))]
        edge, following = own_lines[slot]

        def given(source, near):
            slopes = {at: coef[k] * jnp.maximum(source[0] - near[at[0]][at[1]], 0.0) for k, at in enumerate(OFFSETS)}
            share = jnp.where(outermost, 0.0, 1.0 / (functools.reduce(jnp.add, slopes.values()) + RETENTION))
            return {at: slopes[at] * share for at in slopes}

        def spread(flux, row_step):
            west, east = beside_line(flux[row_step, 1], -1), beside_line(flux[row_step, -1], 1)
            kept = jnp.where(first, 0.0, west) + jnp.where(last, 0.0, east)
            if row_step != 0:
                kept = kept + flux[row_step, 0]
            return kept, jnp.where(first, west, jnp.where(last, east, 0.0))

        from_outside = given(outside[0], {inward: edge, 0: outside[0], -inward: outside[1]})
        from_edge = given(edge, {inward: following, 0: edge, -inward: outside[0]})
        row_at = 0 if slot == 1 else rows - 1
        for values, refs, at in (
                (spread(from_outside, inward), (inner_edge, outer_edge),
                 pl.ds(number * blocks * groups + (0 if slot == 1 else groups - 1), blocks, stride=groups)),
                (spread(from_edge, 0), (inner, outer), pl.ds(row_at, blocks, stride=rows)),
                (spread(from_edge, inward), (inner, outer), pl.ds(row_at + inward, blocks, stride=rows))):
            for value, ref in zip(values, refs):
                ref[at, :] = ref[at, :] + value

    def column(own, left, right):
        beside = jnp.where(sub < 2, pltpu.roll(left, 4, 0), pltpu.roll(right, 4, 0))
        return jnp.where(jnp.logical_and(sub >= 2, sub < 6), own, beside)

    def edge_columns():
        side_tile = [srecv[k, crows:crows + 8, :] for k in range(8)]
        tall_tile = [vrecv[slot, tile_at[slot]:tile_at[slot] + 8, :] for slot in range(2)]
        tile = tall[16 + 2 * crows:24 + 2 * crows, :]
        below = column(tall_tile[0], side_tile[3], side_tile[1])
        above = column(tall_tile[1], side_tile[5], side_tile[7])
        ze = jnp.concatenate([column(tile, side_tile[4], side_tile[0]), jnp.where(lane < half, below, above)], axis=1)
        sub_e = lax.broadcasted_iota(jnp.int32, (8, 2 * LANES), 0)
        beside_e = {step: turn(ze, step, 1) for step in (-1, 0, 1)}
        flux = {}
        for k, (off_row, off_col) in enumerate(OFFSETS):
            flux[off_row, off_col] = coef[k] * jnp.maximum(ze - turn(beside_e[off_row], off_col, 0), 0.0)
        share_e = 1.0 / (functools.reduce(jnp.add, flux.values()) + RETENTION)

        def lines_of(off_row):
            right, left = flux[off_row, 1] * share_e, flux[off_row, -1] * share_e
            picked = jnp.where(sub_e == 1, right, jnp.where(sub_e == 6, left, 0.0))
            picked = jnp.where(sub_e == 3, pltpu.roll(right, 1, 0), jnp.where(sub_e == 4, pltpu.roll(left, 7, 0), picked))
            if off_row == 0:
                return picked
            return jnp.where(jnp.logical_or(sub_e == 2, sub_e == 5), flux[off_row, 0] * share_e, picked)

        from_above = turn(lines_of(1), -1, 1)[:, :LANES]
        from_below = turn(lines_of(-1), 1, 1)[:, :LANES]
        inside = lines_of(0)[:, :LANES] + jnp.where(first, 0.0, from_above) + jnp.where(last, 0.0, from_below)
        outside = jnp.where(first, from_above, jnp.where(last, from_below, 0.0))
        return inside, outside

    picks = jnp.concatenate([where_lane for where_lane in (
        jnp.where(jnp.logical_or(jnp.logical_and(sub < 4, lane == sub - 2), jnp.logical_and(sub >= 4, lane == sub + (LANES - 6))),
                  jnp.where(jnp.logical_and(sub >= 2, sub < 6), 1.0, 0.0), 0.0),
        jnp.where(jnp.logical_or(jnp.logical_and(sub == 1, lane == 0), jnp.logical_and(sub == 6, lane == LANES - 1)), 1.0, 0.0))], axis=1)
    picks = jnp.concatenate([picks] * 3, axis=0).astype(jnp.bfloat16)

    def upright(lines):
        high = lines.astype(jnp.bfloat16)
        rest = lines - high.astype(F32)
        middle = rest.astype(jnp.bfloat16)
        low = (rest - middle.astype(F32)).astype(jnp.bfloat16)
        split = jnp.concatenate([high.astype(F32), middle.astype(F32), low.astype(F32)], axis=0)
        return jnp.dot(jnp.transpose(split).astype(jnp.bfloat16), picks, preferred_element_type=F32)

    def add_inside(values):
        for field, start in ((inner, 0), (outer, LANES)):
            for g in range(groups):
                value = values[8 * g:8 * g + 8, start:start + LANES]
                for j, chosen in ((0, jnp.where(lane < half, value, 0.0)), (far, jnp.where(lane < half, 0.0, value))):
                    at = pl.ds(j * rows + 8 * g, 8)
                    field[at, :] = field[at, :] + chosen

    def add_outside(values):
        for which, field in enumerate((inner_edge, outer_edge)):
            turned[which] = values[:, which * LANES:(which + 1) * LANES]
            for number in range(2):
                for h in range(halves):
                    value = turned[which, pl.ds(64 * h + 7 * number, 8, stride=8), :]
                    for j, chosen in ((0, jnp.where(lane < half, value, 0.0)), (far, jnp.where(lane < half, 0.0, value))):
                        at = edge_at(number, j, h)
                        field[at, :] = field[at, :] + chosen

    def sent(k):
        @pl.when(exists[k])
        def _():
            copies(k).wait_send()

    flow = sweep(flow)
    sent(0)
    inside, outside = edge_columns()
    flow = sweep(flow)
    edge_row(0)
    flow = sweep(flow)
    sent(1)
    upright_inside, upright_outside = upright(inside), upright(outside)
    flow = sweep(flow)
    edge_row(1)
    flow = sweep(flow)
    flow = sweep(flow)
    sent(2)
    add_inside(upright_inside)
    add_outside(upright_outside)
    flow = sweep(flow)
    for k in range(3, 8):
        sent(k)

    flow_ref[...] = flow


def finish(flow_ref, base, inner, outer, inner_edge, outer_edge, out_ref, result, sem):
    blocks, rows, _ = base.shape
    groups, far = rows // 8, blocks - 1
    halves = groups // 8
    lane = lax.broadcasted_iota(jnp.int32, (8, LANES), 1)
    sub = lax.broadcasted_iota(jnp.int32, (8, LANES), 0)
    first, last = (lane & 7) == 0, (lane & 7) == 7
    per_block = LANES // 8
    aside = jnp.where(first, -1, jnp.where(last, 1, 0))
    flow = [flow_ref[8 * h:8 * h + 8, :] for h in range(halves + 2)]
    beyond = jnp.where(lax.broadcasted_iota(jnp.int32, (8, 2 * LANES), 0) < 4, flow[halves], flow[halves + 1])
    places = [(x[:, :LANES], x[:, LANES:]) for x in flow[:halves] + [beyond]]
    copies = [
        pltpu.make_async_copy(result.at[j], out_ref.at[:, pl.ds(j * LANES, LANES)], sem.at[j]) for j in range(blocks)]
    for j in range(blocks):
        index = lane // 8 + j * per_block
        spread = []
        for centre, other in places:
            beside = take_lanes(centre, jnp.clip(index + aside, 0, LANES - 1))
            if j == 0:
                beside = jnp.where(lane == 0, pltpu.roll(other, 1, 1), beside)
            if j == far:
                beside = jnp.where(lane == LANES - 1, pltpu.roll(other, LANES - 1, 1), beside)
            spread.append((take_lanes(centre, index), beside))
        for g in range(groups):
            def level(number):
                return jnp.broadcast_to(spread[g // 8][number][g % 8:g % 8 + 1, :], (8, LANES))

            at, flat = pl.ds(8 * g, 8), pl.ds(j * rows + 8 * g, 8)
            result[j, at, :] = base[j, at, :] + inner[flat, :] * level(0) + outer[flat, :] * level(1)
        for h in range(halves):
            for number in range(2):
                terms = []
                for which in range(2):
                    here = spread[h][which]
                    if number == 0:
                        other = spread[h - 1][which] if h > 0 else spread[-1][which]
                        level = jnp.where(sub == 0, pltpu.roll(other, 1, 0), pltpu.roll(here, 1, 0))
                    else:
                        other = spread[h + 1][which] if h < halves - 1 else spread[-1][which]
                        level = jnp.where(sub == 7, pltpu.roll(other, 7, 0), pltpu.roll(here, 7, 0))
                    flat = pl.ds((number * blocks + j) * groups + 8 * h, 8)
                    terms.append((inner_edge, outer_edge)[which][flat, :] * level)
                at = pl.ds(64 * h + 7 * number, 8, stride=8)
                result[j, at, :] = result[j, at, :] + (terms[0] + terms[1])
        copies[j].start()
    for copy in copies:
        copy.wait()


def solution(mesh):
    row_devices, col_devices = mesh.shape["rows"], mesh.shape["cols"]

    def on_device(elevation, data_mask, tie_order):
        rows, cols = elevation.shape
        groups, blocks = rows // 8, cols // LANES
        tall = 24 + 2 * groups
        vmem = pl.BlockSpec(memory_space=pltpu.VMEM)
        fields = [
            (2 * groups, 2 * LANES), (blocks, rows, LANES), (blocks * rows, LANES), (blocks * rows, LANES),
            (2 * blocks * groups, LANES), (2 * blocks * groups, LANES)]
        given = pl.pallas_call(
            functools.partial(exchange, row_devices, col_devices),
            out_shape=[pltpu.VMEM(shape, F32) for shape in fields],
            in_specs=[pl.BlockSpec(memory_space=pl.ANY)] * 3,
            out_specs=[vmem] * len(fields),
            scratch_shapes=[
                pltpu.SMEM((8,), jnp.int32),
                pltpu.VMEM((blocks, rows + 16, LANES), F32),
                pltpu.VMEM((blocks, rows + 16, LANES), F32),
                pltpu.VMEM((blocks, rows + 16, LANES), F32),
                pltpu.VMEM((blocks, rows, LANES), jnp.int32),
                pltpu.VMEM((blocks, rows + 16, LANES), F32),
                pltpu.VMEM((2, rows, LANES), F32),
                pltpu.VMEM((cols, 2 * LANES), jnp.bfloat16),
                pltpu.VMEM((4 * groups, cols), jnp.bfloat16),
                pltpu.VMEM((groups + 8, LANES), F32),
                pltpu.VMEM((tall + 16, LANES), F32),
                pltpu.VMEM((8, groups + 8, LANES), F32),
                pltpu.VMEM((2, tall, LANES), F32),
                pltpu.SemaphoreType.DMA((2 * blocks,)),
                pltpu.SemaphoreType.DMA,
                pltpu.SemaphoreType.DMA((8,)),
                pltpu.SemaphoreType.DMA((8,)),
            ],
            compiler_params=pltpu.CompilerParams(collective_id=0, has_side_effects=True, vmem_limit_bytes=61000000),
        )(tie_order, elevation, data_mask)
        return pl.pallas_call(
            finish,
            out_shape=jax.ShapeDtypeStruct((rows, cols), F32),
            in_specs=[vmem] * len(fields),
            out_specs=pl.BlockSpec(memory_space=pl.ANY),
            scratch_shapes=[pltpu.VMEM((blocks, rows, LANES), F32), pltpu.SemaphoreType.DMA((blocks,))],
            compiler_params=pltpu.CompilerParams(vmem_limit_bytes=40000000),
        )(*given)

    return jax.shard_map(
        on_device, mesh=mesh, in_specs=(P("rows", "cols"), P("rows", "cols"), P()),
        out_specs=P("rows", "cols"), check_vma=False)
```

time: 9.34 us -> 9.05 us (0.969)
  local copies, waits for them, and re-layouts: 0.8 us -> 0 us
  Pallas kernels: 8.37 us -> 8.87 us
    unnamed x1 -> x0, local copies, waits for them, and re-layouts: 0.8 us -> none
    pallas_call x1 -> x2, Pallas kernels: 8.37 us -> 8.87 us  [the longest x1 7.9 us: on_device(): pl.pallas_call(functools.partial(exchange, row_devices, col_devices), out...]
where the time goes in v3:
time: 9.05 us; the launch traced here: 8.88 us
  Pallas kernels  8.87 us (98%)
    pallas_call x1, Pallas kernels, on_device(): pl.pallas_call(functools.partial(exchange, row_devices, col_devices), out...  7.9 us
    pallas_call x1, Pallas kernels, on_device(): pl.pallas_call(finish, out_shape=jax.ShapeDtypeStruct((rows, cols), F32),...  0.97 us

profile of v3, /device:TPU:0, one launch (start us, length us, event | category | flops | bytes accessed | tf_op | source)
XLA Modules:
  0.0 8.9 jit_solution(14735570426826955947)
XLA Ops:
  0.0 7.9 %shard_map.37 = (f32[32,256]{1,0:T(8,128)S(1)}, f32[8,128,128]{2,1,0:T(8,128)S(1)}, f32[1024,128]{1,0:T(8,128)S(1)}, f32[1024,128]{1,0:T(8,128)S(1)}, f32[256,128]{1,0:T(8,128)S(1)}, /*index=5*/f32[256,128]{1,0:T(8,128)S(1)}) custom-call(s32[8]{0:T(128)} %tie_hbm.1, f32[128,1024]{1,0:T(8,128)} %elev_ref.1, s32[128,1024]{1,0:T(8,128)} %mask_ref.1), custom_call_target="tpu_custom_call" | custom-call | tf_op jit(solution)/shard_map/pallas_call | solution.py:498
  7.9 1.0 %shard_map.38 = f32[128,1024]{1,0:T(8,128)} custom-call(f32[32,256]{1,0:T(8,128)S(1)} %get-tuple-element.11.flow_ref, f32[8,128,128]{2,1,0:T(8,128)S(1)} %get-tuple-element.12.base, f32[1024,128]{1,0:T(8,128)S(1)} %get-tuple-element.13.inner, f32[1024,128]{1,0:T(8,128)S(1)} %get-tuple-element.14.outer, f32[256,128]{1,0:T(8,128)S(1)} %get-tuple-element.15.inner_edge, ...), custom_call_target="tpu_custom_call" | custom-call | tf_op jit(solution)/shard_map/pallas_call | solution.py:524

commit v4 on v3

--- a/solution.py
+++ b/solution.py
@@ -51,12 +51,11 @@
     for j in [0, far] + list(range(1, far)):
         part = pl.ds(j * LANES, LANES)
         loads[j] = (
-            pltpu.make_async_copy(elev_ref.at[:, part], zp.at[j, pl.ds(8, rows), :], load_sem.at[j]),
-            pltpu.make_async_copy(mask_ref.at[:, part], mask.at[j], load_sem.at[blocks + j]))
+            pltpu.make_async_copy(elev_ref.at[:, part], zp.at[j, pl.ds(8, rows), :], load_sem.at[0 if j in (0, far) else 1]),
+            pltpu.make_async_copy(mask_ref.at[:, part], mask.at[j], load_sem.at[0 if j in (0, far) else 2]))
+    for j in (0, far):
         loads[j][0].start()
         loads[j][1].start()
-    tie_load = pltpu.make_async_copy(tie_hbm, tie_ref, tie_sem)
-    tie_load.start()
 
     barrier = pltpu.get_barrier_semaphore()
     exists = []
@@ -75,10 +74,16 @@
     def peer(k):
         return {"rows": row + OFFSETS[k][0], "cols": col + OFFSETS[k][1]}
 
-    for k in range(8):
+    for k in (5, 6, 4, 7, 3, 2, 1, 0):
         @pl.when(exists[k])
         def _():
             pl.semaphore_signal(barrier, inc=1, device_id=peer(k), device_id_type=pl.DeviceIdType.MESH)
+
+    for j in range(1, far):
+        loads[j][0].start()
+        loads[j][1].start()
+    tie_load = pltpu.make_async_copy(tie_hbm, tie_ref, tie_sem)
+    tie_load.start()
 
     lane = lax.broadcasted_iota(jnp.int32, (8, LANES), 1)
     sub = lax.broadcasted_iota(jnp.int32, (8, LANES), 0)
@@ -92,8 +97,13 @@
 
     taker = lax.broadcasted_iota(jnp.int32, (cols, LANES), 1)
     giver = lax.broadcasted_iota(jnp.int32, (cols, LANES), 0) // 8
-    ones[:, :LANES] = (giver == taker).astype(F32).astype(jnp.bfloat16)
-    ones[:, LANES:] = (giver == (taker ^ half)).astype(F32).astype(jnp.bfloat16)
+
+    def chosen(here, wanted):
+        return (here == wanted).astype(F32).astype(jnp.bfloat16)
+
+    ones[0:cols, :] = chosen(giver, taker)
+    for part, start in ((0, 0), (1, far * LANES)):
+        ones[cols + part * LANES:cols + (part + 1) * LANES, :] = chosen(giver[start:start + LANES], taker[0:LANES] ^ half)
 
     order = list(loads)
 
@@ -114,27 +124,28 @@
                 line = (0, 8, 24 + 2 * crows, 32 + 2 * crows)[number]
                 tall[line + j:line + j + 1, :] = zp[j, at:at + 1, :]
 
-    for part in [order[at:at + 2] for at in range(0, blocks, 2)]:
-        for j in part:
-            loads[j][0].wait()
-            loads[j][1].wait()
-        if 0 in part:
-            ends = jnp.where(lax.broadcasted_iota(jnp.int32, (rows, LANES), 1) < half, zp[0, 8:8 + rows, :], zp[far, 8:8 + rows, :])
-            ends = jnp.transpose(ends)
-            tile = jnp.where(sub < 4, pltpu.roll(ends[0:8], 2, 0), pltpu.roll(ends[LANES - 8:LANES], 6, 0))
-            tall[16 + 2 * crows:24 + 2 * crows, :] = tile
-            side[crows:crows + 8, :] = tile
-        row_sums(part)
-    both = jnp.dot(sums[...], ones[...], preferred_element_type=F32)
-    total = both[:, :LANES]
-    counts = total[0:crows]
-    heights = total[crows:2 * crows] + (total[2 * crows:3 * crows] + total[3 * crows:])
-    overview = heights / (counts + 1.0)
-    runoff = counts * (1.0 / 64.0)
-    tall[16:16 + crows, :] = overview
-    tall[16 + crows:16 + 2 * crows, :] = runoff
-
-    side[0:crows, :] = jnp.where(middle_lanes, both[0:crows, LANES:] * (1.0 / 64.0), overview)
+    def loaded(number, count):
+        whole = mask.at[pl.ds(0, count)]
+        pltpu.make_async_copy(whole, whole, load_sem.at[number]).wait()
+
+    loaded(0, 4)
+    ends = jnp.where(lax.broadcasted_iota(jnp.int32, (rows, LANES), 1) < half, zp[0, 8:8 + rows, :], zp[far, 8:8 + rows, :])
+    ends = jnp.transpose(ends)
+    tile = jnp.where(sub < 4, pltpu.roll(ends[0:8], 2, 0), pltpu.roll(ends[LANES - 8:LANES], 6, 0))
+    tall[16 + 2 * crows:24 + 2 * crows, :] = tile
+    side[crows:crows + 8, :] = tile
+    row_sums((0, far))
+
+    def levels(total):
+        counts = total[0:crows]
+        heights = total[crows:2 * crows] + (total[2 * crows:3 * crows] + total[3 * crows:])
+        return heights / (counts + 1.0), counts * (1.0 / 64.0)
+
+    at_ends = jnp.concatenate([sums[:, 0:LANES], sums[:, far * LANES:]], axis=1)
+    from_ends = jnp.concatenate([ones[0:LANES, :], ones[far * LANES:cols, :]], axis=0)
+    overview, _ = levels(jnp.dot(at_ends, from_ends, preferred_element_type=F32))
+    turned_counts = jnp.dot(at_ends[0:crows], ones[cols:, :], preferred_element_type=F32)
+    side[0:crows, :] = jnp.where(middle_lanes, turned_counts * (1.0 / 64.0), overview)
 
     pl.semaphore_wait(barrier, functools.reduce(jnp.add, [there.astype(jnp.int32) for there in exists]))
 
@@ -145,13 +156,25 @@
         else:
             src, dst = side, srecv.at[slot]
         return pltpu.make_async_remote_copy(
-            src_ref=src, dst_ref=dst, send_sem=send_sem.at[k], recv_sem=recv_sem.at[slot],
+            src_ref=src, dst_ref=dst, send_sem=send_sem.at[k % 4 // 2 if k in UPDOWN else 0], recv_sem=recv_sem,
             device_id=peer(k), device_id_type=pl.DeviceIdType.MESH)
 
-    for k in (5, 4, 6, 7, 3, 1, 0, 2):
-        @pl.when(exists[k])
-        def _():
-            copies(k).start()
+    def send(ks):
+        for k in ks:
+            @pl.when(exists[k])
+            def _():
+                copies(k).start()
+
+    send((5, 4, 7, 3, 1, 0))
+
+    for number in (1, 2):
+        loaded(number, blocks - 2)
+    row_sums(order[2:])
+    overview, runoff = levels(jnp.dot(sums[...], ones[0:cols, :], preferred_element_type=F32))
+    tall[16:16 + crows, :] = overview
+    tall[16 + crows:16 + 2 * crows, :] = runoff
+
+    send((6, 2))
 
     for k in range(8):
         @pl.when(jnp.logical_not(exists[k]))
@@ -243,10 +266,22 @@
         for h in range(halves):
             compact(number, way, h)
 
-    for k in range(8):
-        @pl.when(exists[k])
-        def _():
-            copies(k, arriving=True).wait_recv()
+    along_rows, along_cols = [
+        exists[a].astype(jnp.int32) + exists[b].astype(jnp.int32) for a, b in ((2, 6), (0, 4))]
+
+    def all_of(sem, sides, updown):
+        for a in range(min(row_devices - 1, 1), min(row_devices - 1, 2) + 1):
+            for b in range(min(col_devices - 1, 1), min(col_devices - 1, 2) + 1):
+                lines = sides * (crows + 8) * (b + a * b) + updown * (24 + 2 * crows) * a
+                if lines > 0:
+                    @pl.when(jnp.logical_and(along_rows == a, along_cols == b))
+                    def _():
+                        part = turned.at[pl.ds(0, lines), :]
+                        pltpu.make_async_copy(part, part, sem).wait()
+
+    all_of(send_sem.at[0], 1, 0)
+    all_of(send_sem.at[1], 0, 1)
+    all_of(recv_sem, 1, 1)
 
     def turn(x, step, axis):
         return x if step == 0 else pltpu.roll(x, (-step) % x.shape[axis], axis)
@@ -399,37 +434,27 @@
 
     def add_outside(values):
         for which, field in enumerate((inner_edge, outer_edge)):
-            turned[which] = values[:, which * LANES:(which + 1) * LANES]
+            turned[which * rows:(which + 1) * rows, :] = values[:, which * LANES:(which + 1) * LANES]
             for number in range(2):
                 for h in range(halves):
-                    value = turned[which, pl.ds(64 * h + 7 * number, 8, stride=8), :]
+                    value = turned[pl.ds(which * rows + 64 * h + 7 * number, 8, stride=8), :]
                     for j, chosen in ((0, jnp.where(lane < half, value, 0.0)), (far, jnp.where(lane < half, 0.0, value))):
                         at = edge_at(number, j, h)
                         field[at, :] = field[at, :] + chosen
 
-    def sent(k):
-        @pl.when(exists[k])
-        def _():
-            copies(k).wait_send()
-
-    flow = sweep(flow)
-    sent(0)
+    flow = sweep(flow)
     inside, outside = edge_columns()
     flow = sweep(flow)
     edge_row(0)
     flow = sweep(flow)
-    sent(1)
     upright_inside, upright_outside = upright(inside), upright(outside)
     flow = sweep(flow)
     edge_row(1)
     flow = sweep(flow)
     flow = sweep(flow)
-    sent(2)
     add_inside(upright_inside)
     add_outside(upright_outside)
     flow = sweep(flow)
-    for k in range(3, 8):
-        sent(k)
 
     flow_ref[...] = flow
 
@@ -447,7 +472,7 @@
     beyond = jnp.where(lax.broadcasted_iota(jnp.int32, (8, 2 * LANES), 0) < 4, flow[halves], flow[halves + 1])
     places = [(x[:, :LANES], x[:, LANES:]) for x in flow[:halves] + [beyond]]
     copies = [
-        pltpu.make_async_copy(result.at[j], out_ref.at[:, pl.ds(j * LANES, LANES)], sem.at[j]) for j in range(blocks)]
+        pltpu.make_async_copy(result.at[j], out_ref.at[:, pl.ds(j * LANES, LANES)], sem) for j in range(blocks)]
     for j in range(blocks):
         index = lane // 8 + j * per_block
         spread = []
@@ -480,8 +505,7 @@
                 at = pl.ds(64 * h + 7 * number, 8, stride=8)
                 result[j, at, :] = result[j, at, :] + (terms[0] + terms[1])
         copies[j].start()
-    for copy in copies:
-        copy.wait()
+    pltpu.make_async_copy(result, result, sem).wait()
 
 
 def solution(mesh):
@@ -507,17 +531,17 @@
                 pltpu.VMEM((blocks, rows + 16, LANES), F32),
                 pltpu.VMEM((blocks, rows, LANES), jnp.int32),
                 pltpu.VMEM((blocks, rows + 16, LANES), F32),
-                pltpu.VMEM((2, rows, LANES), F32),
-                pltpu.VMEM((cols, 2 * LANES), jnp.bfloat16),
+                pltpu.VMEM((2 * rows + 16 * groups, LANES), F32),
+                pltpu.VMEM((cols + 2 * LANES, LANES), jnp.bfloat16),
                 pltpu.VMEM((4 * groups, cols), jnp.bfloat16),
                 pltpu.VMEM((groups + 8, LANES), F32),
                 pltpu.VMEM((tall + 16, LANES), F32),
                 pltpu.VMEM((8, groups + 8, LANES), F32),
                 pltpu.VMEM((2, tall, LANES), F32),
-                pltpu.SemaphoreType.DMA((2 * blocks,)),
+                pltpu.SemaphoreType.DMA((3,)),
                 pltpu.SemaphoreType.DMA,
-                pltpu.SemaphoreType.DMA((8,)),
-                pltpu.SemaphoreType.DMA((8,)),
+                pltpu.SemaphoreType.DMA((2,)),
+                pltpu.SemaphoreType.DMA,
             ],
             compiler_params=pltpu.CompilerParams(collective_id=0, has_side_effects=True, vmem_limit_bytes=61000000),
         )(tie_order, elevation, data_mask)
@@ -526,7 +550,7 @@
             out_shape=jax.ShapeDtypeStruct((rows, cols), F32),
             in_specs=[vmem] * len(fields),
             out_specs=pl.BlockSpec(memory_space=pl.ANY),
-            scratch_shapes=[pltpu.VMEM((blocks, rows, LANES), F32), pltpu.SemaphoreType.DMA((blocks,))],
+            scratch_shapes=[pltpu.VMEM((blocks, rows, LANES), F32), pltpu.SemaphoreType.DMA],
             compiler_params=pltpu.CompilerParams(vmem_limit_bytes=40000000),
         )(*given)
 

time: 9.05 us -> 8.61 us (0.951)
  Pallas kernels: 8.87 us -> 8.44 us
    pallas_call x1, Pallas kernels: 7.9 us -> 7.54 us  [on_device(): pl.pallas_call(functools.partial(exchange, row_devices, col_devices), out...]
where the time goes in v4:
time: 8.61 us; the launch traced here: 8.45 us
  Pallas kernels  8.44 us (98%)
    pallas_call x1, Pallas kernels, on_device(): pl.pallas_call(functools.partial(exchange, row_devices, col_devices), out...  7.54 us
    pallas_call x1, Pallas kernels, on_device(): pl.pallas_call(finish, out_shape=jax.ShapeDtypeStruct((rows, cols), F32),...  0.9 us

profile of v4, /device:TPU:0, one launch (start us, length us, event | category | flops | bytes accessed | tf_op | source)
XLA Modules:
  0.0 8.4 jit_solution(9425207888440137810)
XLA Ops:
  0.0 7.5 %shard_map.37 = (f32[32,256]{1,0:T(8,128)S(1)}, f32[8,128,128]{2,1,0:T(8,128)S(1)}, f32[1024,128]{1,0:T(8,128)S(1)}, f32[1024,128]{1,0:T(8,128)S(1)}, f32[256,128]{1,0:T(8,128)S(1)}, /*index=5*/f32[256,128]{1,0:T(8,128)S(1)}) custom-call(s32[8]{0:T(128)} %tie_hbm.1, f32[128,1024]{1,0:T(8,128)} %elev_ref.1, s32[128,1024]{1,0:T(8,128)} %mask_ref.1), custom_call_target="tpu_custom_call" | custom-call | tf_op jit(solution)/shard_map/pallas_call | solution.py:522
  7.5 0.9 %shard_map.38 = f32[128,1024]{1,0:T(8,128)} custom-call(f32[32,256]{1,0:T(8,128)S(1)} %get-tuple-element.11.flow_ref, f32[8,128,128]{2,1,0:T(8,128)S(1)} %get-tuple-element.12.base, f32[1024,128]{1,0:T(8,128)S(1)} %get-tuple-element.13.inner, f32[1024,128]{1,0:T(8,128)S(1)} %get-tuple-element.14.outer, f32[256,128]{1,0:T(8,128)S(1)} %get-tuple-element.15.inner_edge, ...), custom_call_target="tpu_custom_call" | custom-call | tf_op jit(solution)/shard_map/pallas_call | solution.py:548

commit v5 on v4

--- a/solution.py
+++ b/solution.py
@@ -40,7 +40,7 @@
 
 
 def exchange(row_devices, col_devices, tie_hbm, elev_ref, mask_ref, flow_ref, base, inner, outer, inner_edge, outer_edge,
-             tie_ref, zp, zl, zr, mask, recip, turned, ones, sums, side, tall, srecv, vrecv, load_sem, tie_sem, send_sem, recv_sem):
+             tie_ref, zp, zl, zr, mask, recip, turned, ones, sums, side, tall, srecv, vrecv, load_sem, tie_sem, recv_sem):
     rows, cols = elev_ref.shape
     groups, blocks = rows // 8, cols // LANES
     crows, halves = groups, groups // 8
@@ -52,11 +52,7 @@
         part = pl.ds(j * LANES, LANES)
         loads[j] = (
             pltpu.make_async_copy(elev_ref.at[:, part], zp.at[j, pl.ds(8, rows), :], load_sem.at[0 if j in (0, far) else 1]),
-            pltpu.make_async_copy(mask_ref.at[:, part], mask.at[j], load_sem.at[0 if j in (0, far) else 2]))
-    for j in (0, far):
-        loads[j][0].start()
-        loads[j][1].start()
-
+            pltpu.make_async_copy(mask_ref.at[:, part], mask.at[j], load_sem.at[0 if j in (0, far) else 1]))
     barrier = pltpu.get_barrier_semaphore()
     exists = []
     for step_row, step_col in OFFSETS:
@@ -79,7 +75,7 @@
         def _():
             pl.semaphore_signal(barrier, inc=1, device_id=peer(k), device_id_type=pl.DeviceIdType.MESH)
 
-    for j in range(1, far):
+    for j in loads:
         loads[j][0].start()
         loads[j][1].start()
     tie_load = pltpu.make_async_copy(tie_hbm, tie_ref, tie_sem)
@@ -125,9 +121,10 @@
                 tall[line + j:line + j + 1, :] = zp[j, at:at + 1, :]
 
     def loaded(number, count):
-        whole = mask.at[pl.ds(0, count)]
+        whole = turned.at[pl.ds(0, count * rows), :]
         pltpu.make_async_copy(whole, whole, load_sem.at[number]).wait()
 
+    tie_load.wait()
     loaded(0, 4)
     ends = jnp.where(lax.broadcasted_iota(jnp.int32, (rows, LANES), 1) < half, zp[0, 8:8 + rows, :], zp[far, 8:8 + rows, :])
     ends = jnp.transpose(ends)
@@ -156,7 +153,7 @@
         else:
             src, dst = side, srecv.at[slot]
         return pltpu.make_async_remote_copy(
-            src_ref=src, dst_ref=dst, send_sem=send_sem.at[k % 4 // 2 if k in UPDOWN else 0], recv_sem=recv_sem,
+            src_ref=src, dst_ref=dst, send_sem=tie_sem, recv_sem=recv_sem,
             device_id=peer(k), device_id_type=pl.DeviceIdType.MESH)
 
     def send(ks):
@@ -167,8 +164,7 @@
 
     send((5, 4, 7, 3, 1, 0))
 
-    for number in (1, 2):
-        loaded(number, blocks - 2)
+    loaded(1, 2 * blocks - 4)
     row_sums(order[2:])
     overview, runoff = levels(jnp.dot(sums[...], ones[0:cols, :], preferred_element_type=F32))
     tall[16:16 + crows, :] = overview
@@ -187,7 +183,6 @@
                 srecv[k, 0:crows, :] = jnp.where(middle_lanes, 0.0, OUTSIDE)
                 srecv[k, crows:crows + 8, :] = jnp.full((8, LANES), OUTSIDE, F32)
 
-    tie_load.wait()
     coef = coefficients(tie_ref)
 
     for ref in (zp, zl, zr, recip):
@@ -269,19 +264,18 @@
     along_rows, along_cols = [
         exists[a].astype(jnp.int32) + exists[b].astype(jnp.int32) for a, b in ((2, 6), (0, 4))]
 
-    def all_of(sem, sides, updown):
+    def all_of(sem):
         for a in range(min(row_devices - 1, 1), min(row_devices - 1, 2) + 1):
             for b in range(min(col_devices - 1, 1), min(col_devices - 1, 2) + 1):
-                lines = sides * (crows + 8) * (b + a * b) + updown * (24 + 2 * crows) * a
+                lines = (crows + 8) * (b + a * b) + (24 + 2 * crows) * a
                 if lines > 0:
                     @pl.when(jnp.logical_and(along_rows == a, along_cols == b))
                     def _():
                         part = turned.at[pl.ds(0, lines), :]
                         pltpu.make_async_copy(part, part, sem).wait()
 
-    all_of(send_sem.at[0], 1, 0)
-    all_of(send_sem.at[1], 0, 1)
-    all_of(recv_sem, 1, 1)
+    all_of(tie_sem)
+    all_of(recv_sem)
 
     def turn(x, step, axis):
         return x if step == 0 else pltpu.roll(x, (-step) % x.shape[axis], axis)
@@ -531,16 +525,15 @@
                 pltpu.VMEM((blocks, rows + 16, LANES), F32),
                 pltpu.VMEM((blocks, rows, LANES), jnp.int32),
                 pltpu.VMEM((blocks, rows + 16, LANES), F32),
-                pltpu.VMEM((2 * rows + 16 * groups, LANES), F32),
+                pltpu.VMEM((2 * blocks * rows, LANES), F32),
                 pltpu.VMEM((cols + 2 * LANES, LANES), jnp.bfloat16),
                 pltpu.VMEM((4 * groups, cols), jnp.bfloat16),
                 pltpu.VMEM((groups + 8, LANES), F32),
                 pltpu.VMEM((tall + 16, LANES), F32),
                 pltpu.VMEM((8, groups + 8, LANES), F32),
                 pltpu.VMEM((2, tall, LANES), F32),
-                pltpu.SemaphoreType.DMA((3,)),
+                pltpu.SemaphoreType.DMA((2,)),
                 pltpu.SemaphoreType.DMA,
-                pltpu.SemaphoreType.DMA((2,)),
                 pltpu.SemaphoreType.DMA,
             ],
             compiler_params=pltpu.CompilerParams(collective_id=0, has_side_effects=True, vmem_limit_bytes=61000000),

time: 8.61 us -> 8.58 us (level)
  no operation moved by 1% of the time
where the time goes in v5:
time: 8.58 us; the launch traced here: 8.42 us
  Pallas kernels  8.41 us (98%)
    pallas_call x1, Pallas kernels, on_device(): pl.pallas_call(functools.partial(exchange, row_devices, col_devices), out...  7.51 us
    pallas_call x1, Pallas kernels, on_device(): pl.pallas_call(finish, out_shape=jax.ShapeDtypeStruct((rows, cols), F32),...  0.9 us

profile of v5, /device:TPU:0, one launch (start us, length us, event | category | flops | bytes accessed | tf_op | source)
XLA Modules:
  0.0 8.4 jit_solution(17425283801065200642)
XLA Ops:
  0.0 7.5 %shard_map.37 = (f32[32,256]{1,0:T(8,128)S(1)}, f32[8,128,128]{2,1,0:T(8,128)S(1)}, f32[1024,128]{1,0:T(8,128)S(1)}, f32[1024,128]{1,0:T(8,128)S(1)}, f32[256,128]{1,0:T(8,128)S(1)}, /*index=5*/f32[256,128]{1,0:T(8,128)S(1)}) custom-call(s32[8]{0:T(128)} %tie_hbm.1, f32[128,1024]{1,0:T(8,128)} %elev_ref.1, s32[128,1024]{1,0:T(8,128)} %mask_ref.1), custom_call_target="tpu_custom_call" | custom-call | tf_op jit(solution)/shard_map/pallas_call | solution.py:516
  7.5 0.9 %shard_map.38 = f32[128,1024]{1,0:T(8,128)} custom-call(f32[32,256]{1,0:T(8,128)S(1)} %get-tuple-element.11.flow_ref, f32[8,128,128]{2,1,0:T(8,128)S(1)} %get-tuple-element.12.base, f32[1024,128]{1,0:T(8,128)S(1)} %get-tuple-element.13.inner, f32[1024,128]{1,0:T(8,128)S(1)} %get-tuple-element.14.outer, f32[256,128]{1,0:T(8,128)S(1)} %get-tuple-element.15.inner_edge, ...), custom_call_target="tpu_custom_call" | custom-call | tf_op jit(solution)/shard_map/pallas_call | solution.py:541

commit v6 on v5

--- a/solution.py
+++ b/solution.py
@@ -103,6 +103,9 @@
 
     order = list(loads)
 
+    def turn(x, step, axis):
+        return x if step == 0 else pltpu.roll(x, (-step) % x.shape[axis], axis)
+
     def row_sums(some):
         for j in some:
             height_sum = jnp.zeros((crows, LANES), F32)
@@ -130,7 +133,16 @@
     ends = jnp.transpose(ends)
     tile = jnp.where(sub < 4, pltpu.roll(ends[0:8], 2, 0), pltpu.roll(ends[LANES - 8:LANES], 6, 0))
     tall[16 + 2 * crows:24 + 2 * crows, :] = tile
-    side[crows:crows + 8, :] = tile
+    parts = [turn(tile, 32 * c - 16, 1) for c in range(4)]
+
+    def packed(at):
+        value = nothing
+        for c in range(4):
+            value = jnp.where(sub == c, pltpu.roll(parts[c], (c - at) % 8, 0), value)
+            value = jnp.where(sub == c + 4, pltpu.roll(parts[c], (c + 3 - at) % 8, 0), value)
+        return value
+
+    lines = jnp.concatenate([packed(2), packed(4)], axis=0)
     row_sums((0, far))
 
     def levels(total):
@@ -142,7 +154,8 @@
     from_ends = jnp.concatenate([ones[0:LANES, :], ones[far * LANES:cols, :]], axis=0)
     overview, _ = levels(jnp.dot(at_ends, from_ends, preferred_element_type=F32))
     turned_counts = jnp.dot(at_ends[0:crows], ones[cols:, :], preferred_element_type=F32)
-    side[0:crows, :] = jnp.where(middle_lanes, turned_counts * (1.0 / 64.0), overview)
+    side[...] = jnp.where(
+        jnp.logical_and(lane_c >= 16, lane_c < 48), lines, jnp.where(middle_lanes, turned_counts * (1.0 / 64.0), overview))
 
     pl.semaphore_wait(barrier, functools.reduce(jnp.add, [there.astype(jnp.int32) for there in exists]))
 
@@ -180,8 +193,7 @@
                     start = 16 + crows if k == 2 else crows
                     vrecv[k // 4, at:at + 8, :] = jnp.full((8, LANES), 0.0 if start <= at < start + crows else OUTSIDE, F32)
             else:
-                srecv[k, 0:crows, :] = jnp.where(middle_lanes, 0.0, OUTSIDE)
-                srecv[k, crows:crows + 8, :] = jnp.full((8, LANES), OUTSIDE, F32)
+                srecv[k] = jnp.where(jnp.logical_and(lane_c >= 48, lane_c < half + 16), 0.0, OUTSIDE)
 
     coef = coefficients(tie_ref)
 
@@ -267,7 +279,7 @@
     def all_of(sem):
         for a in range(min(row_devices - 1, 1), min(row_devices - 1, 2) + 1):
             for b in range(min(col_devices - 1, 1), min(col_devices - 1, 2) + 1):
-                lines = (crows + 8) * (b + a * b) + (24 + 2 * crows) * a
+                lines = crows * (b + a * b) + (24 + 2 * crows) * a
                 if lines > 0:
                     @pl.when(jnp.logical_and(along_rows == a, along_cols == b))
                     def _():
@@ -276,9 +288,6 @@
 
     all_of(tie_sem)
     all_of(recv_sem)
-
-    def turn(x, step, axis):
-        return x if step == 0 else pltpu.roll(x, (-step) % x.shape[axis], axis)
 
     coarse_at = (16, 0)
     tile_at = (16 + 2 * crows, 2 * crows)
@@ -377,7 +386,17 @@
         return jnp.where(jnp.logical_and(sub >= 2, sub < 6), own, beside)
 
     def edge_columns():
-        side_tile = [srecv[k, crows:crows + 8, :] for k in range(8)]
+        def unpacked(k):
+            start = 2 if OFFSETS[k][1] > 0 else 4
+            given = srecv[k, 0:8, :] if OFFSETS[k][1] > 0 else srecv[k, 8:16, :]
+            value = nothing
+            for c in range(4):
+                moved = turn(given, 16 - 32 * c, 1)
+                pair = jnp.where(sub == start, pltpu.roll(moved, (start - c) % 8, 0), pltpu.roll(moved, (start - 3 - c) % 8, 0))
+                value = jnp.where(lane // 32 == c, pair, value)
+            return value
+
+        side_tile = {k: unpacked(k) for k in SIDES}
         tall_tile = [vrecv[slot, tile_at[slot]:tile_at[slot] + 8, :] for slot in range(2)]
         tile = tall[16 + 2 * crows:24 + 2 * crows, :]
         below = column(tall_tile[0], side_tile[3], side_tile[1])
@@ -528,9 +547,9 @@
                 pltpu.VMEM((2 * blocks * rows, LANES), F32),
                 pltpu.VMEM((cols + 2 * LANES, LANES), jnp.bfloat16),
                 pltpu.VMEM((4 * groups, cols), jnp.bfloat16),
-                pltpu.VMEM((groups + 8, LANES), F32),
+                pltpu.VMEM((groups, LANES), F32),
                 pltpu.VMEM((tall + 16, LANES), F32),
-                pltpu.VMEM((8, groups + 8, LANES), F32),
+                pltpu.VMEM((8, groups, LANES), F32),
                 pltpu.VMEM((2, tall, LANES), F32),
                 pltpu.SemaphoreType.DMA((2,)),
                 pltpu.SemaphoreType.DMA,

time: 8.58 us -> 8.53 us (level)
  no operation moved by 1% of the time
where the time goes in v6:
time: 8.53 us; the launch traced here: 8.37 us
  Pallas kernels  8.36 us (98%)
    pallas_call x1, Pallas kernels, on_device(): pl.pallas_call(functools.partial(exchange, row_devices, col_devices), out...  7.46 us
    pallas_call x1, Pallas kernels, on_device(): pl.pallas_call(finish, out_shape=jax.ShapeDtypeStruct((rows, cols), F32),...  0.9 us

profile of v6, /device:TPU:0, one launch (start us, length us, event | category | flops | bytes accessed | tf_op | source)
XLA Modules:
  0.0 8.4 jit_solution(2853368344997451830)
XLA Ops:
  0.0 7.5 %shard_map.37 = (f32[32,256]{1,0:T(8,128)S(1)}, f32[8,128,128]{2,1,0:T(8,128)S(1)}, f32[1024,128]{1,0:T(8,128)S(1)}, f32[1024,128]{1,0:T(8,128)S(1)}, f32[256,128]{1,0:T(8,128)S(1)}, /*index=5*/f32[256,128]{1,0:T(8,128)S(1)}) custom-call(s32[8]{0:T(128)} %tie_hbm.1, f32[128,1024]{1,0:T(8,128)} %elev_ref.1, s32[128,1024]{1,0:T(8,128)} %mask_ref.1), custom_call_target="tpu_custom_call" | custom-call | tf_op jit(solution)/shard_map/pallas_call | solution.py:535
  7.5 0.9 %shard_map.38 = f32[128,1024]{1,0:T(8,128)} custom-call(f32[32,256]{1,0:T(8,128)S(1)} %get-tuple-element.11.flow_ref, f32[8,128,128]{2,1,0:T(8,128)S(1)} %get-tuple-element.12.base, f32[1024,128]{1,0:T(8,128)S(1)} %get-tuple-element.13.inner, f32[1024,128]{1,0:T(8,128)S(1)} %get-tuple-element.14.outer, f32[256,128]{1,0:T(8,128)S(1)} %get-tuple-element.15.inner_edge, ...), custom_call_target="tpu_custom_call" | custom-call | tf_op jit(solution)/shard_map/pallas_call | solution.py:560

commit v7 on v6

--- a/solution.py
+++ b/solution.py
@@ -318,7 +318,8 @@
     slopes = []
     for k, (step_row, step_col) in enumerate(OFFSETS):
         slopes.append(coef[k] * jnp.maximum(beside_z[0] - turn(beside_z[step_col], step_row, 0), 0.0))
-    share = 1.0 / (functools.reduce(jnp.add, slopes) + RETENTION)
+    pairs = [slopes[k] + slopes[k + 4] for k in range(4)]
+    share = 1.0 / ((pairs[0] + pairs[1]) + (pairs[2] + (pairs[3] + RETENTION)))
 
     def core(x):
         return jnp.concatenate([x[0:crows + 8], x[crows + 16:]], axis=0)
@@ -329,7 +330,7 @@
         source = slopes[k] * share
         given[step_col] = given[step_col] + turn(source * supply, -step_row, 0)
         weight[step_row, step_col] = source
-    flow = core(supply + given[0] + turn(given[1], -1, 1) + turn(given[-1], 1, 1))
+    flow = core((supply + given[0]) + (turn(given[1], -1, 1) + turn(given[-1], 1, 1)))
     weight = {at: turn(core(weight[at]), -at[1], 1) for at in weight}
     supply = core(supply)
 
@@ -339,7 +340,7 @@
         for step_row in (-1, 0, 1):
             sums[step_row] = functools.reduce(
                 jnp.add, [weight[step_row, c] * moved[c] for c in (-1, 0, 1) if (step_row, c) in weight])
-        return supply + sums[0] + turn(sums[1], -1, 0) + turn(sums[-1], 1, 0)
+        return (supply + sums[0]) + (turn(sums[1], -1, 0) + turn(sums[-1], 1, 0))
 
     def beside_line(x, step):
         moved = pltpu.roll(x, 1 if step < 0 else LANES - 1, 1)

time: 8.53 us -> 8.54 us (level)
  no operation moved by 1% of the time
where the time goes in v7:
time: 8.54 us; the launch traced here: 8.38 us
  Pallas kernels  8.37 us (98%)
    pallas_call x1, Pallas kernels, on_device(): pl.pallas_call(functools.partial(exchange, row_devices, col_devices), out...  7.47 us
    pallas_call x1, Pallas kernels, on_device(): pl.pallas_call(finish, out_shape=jax.ShapeDtypeStruct((rows, cols), F32),...  0.9 us

profile of v7, /device:TPU:0, one launch (start us, length us, event | category | flops | bytes accessed | tf_op | source)
XLA Modules:
  0.0 8.4 jit_solution(11731374372642628886)
XLA Ops:
  0.0 7.5 %shard_map.37 = (f32[32,256]{1,0:T(8,128)S(1)}, f32[8,128,128]{2,1,0:T(8,128)S(1)}, f32[1024,128]{1,0:T(8,128)S(1)}, f32[1024,128]{1,0:T(8,128)S(1)}, f32[256,128]{1,0:T(8,128)S(1)}, /*index=5*/f32[256,128]{1,0:T(8,128)S(1)}) custom-call(s32[8]{0:T(128)} %tie_hbm.1, f32[128,1024]{1,0:T(8,128)} %elev_ref.1, s32[128,1024]{1,0:T(8,128)} %mask_ref.1), custom_call_target="tpu_custom_call" | custom-call | tf_op jit(solution)/shard_map/pallas_call | solution.py:536
  7.5 0.9 %shard_map.38 = f32[128,1024]{1,0:T(8,128)} custom-call(f32[32,256]{1,0:T(8,128)S(1)} %get-tuple-element.11.flow_ref, f32[8,128,128]{2,1,0:T(8,128)S(1)} %get-tuple-element.12.base, f32[1024,128]{1,0:T(8,128)S(1)} %get-tuple-element.13.inner, f32[1024,128]{1,0:T(8,128)S(1)} %get-tuple-element.14.outer, f32[256,128]{1,0:T(8,128)S(1)} %get-tuple-element.15.inner_edge, ...), custom_call_target="tpu_custom_call" | custom-call | tf_op jit(solution)/shard_map/pallas_call | solution.py:561
